TPU v7x, 32 devices: a 4x4x1 block of a 4x4x8 slice. The times are simulated.
32 devices in a mesh: dp: 1 (over z), ep: 32 (over y, x, core).
Axes of the slice: x: 4, y: 4, z: 1, core: 2. Of those that a mesh axis runs over, the one named last changes fastest.
The devices are a block of a 4x4x8 slice.
Arguments:
- x_rows: bfloat16 [131072, 1024], P(('dp', 'ep'))
- sel_idx: int32 [32, 8192], P(('dp', 'ep'))
- gate_w: float32 [32, 8192], P(('dp', 'ep'))
- w_up: bfloat16 [32, 1024, 2816], P('ep')
- w_down: bfloat16 [32, 2816, 1024], P('ep')
Outputs:
- output: bfloat16 [131072, 1024], P(('dp', 'ep'))
All inputs are finite; a program needn't handle non-finite values.
Results may differ from a plain program's by a relative error of at most 0.00679449.
Values are sent between devices in bfloat16 or wider.
A program may use at most 768 MiB of HBM per device.

v0:
```python
import jax
import jax.numpy as jnp
from jax import lax
from jax.sharding import PartitionSpec as P


def solution(mesh):
    group_size = mesh.shape["ep"]

    def local_layer(x_loc, sel_loc, gate_loc, up_loc, down_loc):
        tok_loc, model_width = x_loc.shape
        exp_loc, cap_rows = sel_loc.shape
        entry_count = exp_loc * cap_rows
        pair_cap = 2 * entry_count // group_size
        flat_sel = sel_loc.reshape(entry_count)
        src_dev = flat_sel // tok_loc
        local_row = flat_sel - src_dev * tok_loc
        sort_order = jnp.argsort(src_dev, stable=True)
        position = jnp.argsort(sort_order)
        counts = jnp.bincount(src_dev, length=group_size)
        starts = jnp.cumsum(counts) - counts
        slot_idx = src_dev * pair_cap + position - starts[src_dev]
        request = jnp.zeros((group_size * pair_cap,), jnp.int32).at[slot_idx].set(local_row, unique_indices=True)
        wanted = lax.all_to_all(request.reshape(group_size, pair_cap), "ep", 0, 0, tiled=True).reshape(group_size * pair_cap)
        send_rows = jnp.take(x_loc, wanted, axis=0).reshape(group_size, pair_cap, model_width)
        received = lax.all_to_all(send_rows, "ep", 0, 0, tiled=True).reshape(group_size * pair_cap, model_width)
        picked = jnp.take(received, slot_idx, axis=0).reshape(exp_loc, cap_rows, model_width)
        hidden = jax.nn.gelu(jnp.einsum("ecd,edf->ecf", picked, up_loc, preferred_element_type=jnp.float32), approximate=True).astype(jnp.bfloat16)
        out_rows = jnp.einsum("ecf,efd->ecd", hidden, down_loc, preferred_element_type=jnp.float32)
        contrib = (out_rows * gate_loc[:, :, None]).astype(jnp.bfloat16).reshape(entry_count, model_width)
        back_rows = jnp.zeros((group_size * pair_cap, model_width), jnp.bfloat16).at[slot_idx].set(contrib, unique_indices=True)
        returned = lax.all_to_all(back_rows.reshape(group_size, pair_cap, model_width), "ep", 0, 0, tiled=True).reshape(group_size * pair_cap, model_width)
        summed = jax.ops.segment_sum(returned.astype(jnp.float32), wanted, num_segments=tok_loc)
        return (x_loc.astype(jnp.float32) + summed).astype(jnp.bfloat16)

    row_spec = P(("dp", "ep"), None)
    weight_spec = P("ep", None, None)
    return jax.shard_map(local_layer, mesh=mesh, in_specs=(row_spec, row_spec, row_spec, weight_spec, weight_spec), out_specs=row_spec, check_vma=False)
```

profile of v0, /device:TPU:107, one launch (start us, length us, event | category | flops | bytes accessed | tf_op | source)
XLA Modules:
  0.0 1749.4 jit_solution(12414656000882296813)
XLA Ops:
  0.0 0.9 broadcast_maximum_fusion
  0.9 57.0 %scatter_custom_fusion = s32[32]{0:T(128)S(1)} fusion(s32[8192]{0:T(1024)S(1)} %bitcast.98, s32[8192]{0:T(1024)S(1)} %ne.44, s32[]{:T(128)} %constant.26.clone.1), kind=kCustom, calls=%fused_computation.86 | custom fusion | flops 8192 | bytes 132 | tf_op jit(solution)/shard_map/scatter-add | solution.py:20
  57.9 0.1 copy.8
  58.0 0.1 reduce-window.9
  58.1 0.1 reduce.1
  58.2 0.7 fusion.38
  58.9 0.7 fusion.37
  59.7 4.6 compare_select_fusion.3
  64.3 2.5 compare_reduce_fusion.24
  66.8 0.8 multiply_subtract_fusion
  67.6 6.8 sort.34
  74.4 6.8 sort.35
  81.2 17.0 compare_and_fusion.1
  98.2 30.5 %scatter_custom_fusion.1 = s32[16384]{0:T(1024)S(1)} fusion(s32[8192]{0:T(1024)S(1)} %get-tuple-element.37, s32[8192]{0:T(1024)S(1)} %get-tuple-element.42, s32[]{:T(128)} %constant.26.clone.1), kind=kCustom, calls=%fused_computation.79 | custom fusion | bytes 65540 | tf_op jit(solution)/shard_map/scatter | solution.py:23
  128.7 25.6 %all_to_all.19 = s32[32,1,512]{2,1,0:T(1,128)S(1)} all-to-all(s32[32,1,512]{2,1,0:T(1,128)S(1)} %bitcast.95), channel_id=1, replica_groups=mesh['dp'=1,'ep'=32] {'ep'}, dimensions={0} | all-to-all | bytes 131072 | tf_op jit(solution)/shard_map/all_to_all | solution.py:24
  154.2 0.1 compare_select_fusion
  154.3 84.7 %gather_fusion = bf16[16384,1024]{1,0:T(8,128)(2,1)} fusion(bf16[4096,1024]{1,0:T(8,128)(2,1)} %param.5, s32[16384]{0:T(1024)S(1)} %broadcast_clamp_fusion), kind=kCustom, calls=%fused_computation | custom fusion | bytes 67174400 | tf_op jit(solution)/shard_map/jit(_take)/gather | solution.py:25
  239.0 0.0 copy-done
  239.0 22.9 %broadcast_select_fusion = bf16[32,512,1024]{2,1,0:T(8,128)(2,1)} fusion(bf16[32,512,1024]{2,1,0:T(8,128)(2,1)} %bitcast.89, pred[32,512]{1,0:T(8,128)(4,1)S(1)} %compare_and_fusion), kind=kLoop, calls=%fused_computation.19 | loop fusion | flops 16777216 | bytes 67125248 | tf_op jit(solution)/shard_map/jit(_take)/select_n | solution.py:25
  261.9 6.4 all-to-all-start.1
  268.3 6.5 sort.36
  274.8 0.6 broadcast_clamp_fusion.1
  275.5 448.5 %all-to-all-done.1 = bf16[32,512,1024]{2,1,0:T(8,128)(2,1)} async-done(((bf16[32,512,1024]{2,1,0:T(8,128)(2,1)}), bf16[32,512,1024]{2,1,0:T(8,128)(2,1)}, u32[]{:S(2)}, u32[]{:S(2)}) %all-to-all-start.1) | async-done | bytes 33554464 | tf_op jit(solution)/shard_map/all_to_all | solution.py:26
  723.9 150.1 %gather_fusion.1 = bf16[8192,1024]{1,0:T(8,128)(2,1)} fusion(bf16[16384,1024]{1,0:T(8,128)(2,1)} %bitcast.42, s32[8192]{0:T(1024)S(1)} %broadcast_clamp_fusion.2), kind=kCustom, calls=%fused_computation.1 | custom fusion | bytes 33587200 | tf_op jit(solution)/shard_map/jit(_take)/gather | solution.py:27
  874.1 73.6 %fusion.8.clone.4 = bf16[8192,2816]{1,0:T(8,128)(2,1)} fusion(bf16[8192,1024]{1,0:T(8,128)(2,1)} %gather_fusion.1, pred[8192]{0:T(1024)(128)(4,1)S(1)} %copy-done.1, bf16[1,1024,2816]{2,1,0:T(8,128)(2,1)} %param.8), kind=kOutput, calls=%fused_computation.15.clone.clone.clone.1 | convolution fusion | flops 47460646912 | bytes 68689920 | tf_op jit(solution)/shard_map/ecd,edf->ecf/dot_general | solution.py:28
  947.7 55.0 %multiply_convert_fusion = bf16[8192,1024]{1,0:T(8,128)(2,1)} fusion(f32[8192]{0:T(1024)S(1)} %bitcast.100, bf16[1,2816,1024]{2,1,0:T(8,128)(2,1)} %param.9, bf16[8192,2816]{1,0:T(8,128)(2,1)} %fusion.8.clone.4), kind=kOutput, calls=%fused_computation.18 | convolution fusion | flops 47261417472 | bytes 68714496 | tf_op jit(solution)/shard_map/ecf,efd->ecd/dot_general | solution.py:29
  1002.6 131.8 %scatter_custom_fusion.2 = bf16[16384,1024]{1,0:T(8,128)(2,1)} fusion(s32[8192]{0:T(1024)} %get-tuple-element.9, bf16[8192,1024]{1,0:T(8,128)(2,1)} %multiply_convert_fusion, s32[8192]{0:T(1024)} %broadcast_clamp_fusion.1, bf16[]{:T(256)} %constant.63.clone.1), kind=kCustom, calls=%fused_computation.20 | custom fusion | bytes 33554944 | tf_op jit(solution)/shard_map/scatter | solution.py:31
  1134.4 4.7 all-to-all-start.2
  1139.2 11.3 convert_element_type.20
  1150.5 442.2 %all-to-all-done.2 = bf16[32,512,1024]{2,1,0:T(8,128)(2,1)} async-done(((bf16[32,512,1024]{2,1,0:T(8,128)(2,1)}), bf16[32,512,1024]{2,1,0:T(8,128)(2,1)}, u32[]{:S(2)}, u32[]{:S(2)}) %all-to-all-start.2) | async-done | bytes 33554464 | tf_op jit(solution)/shard_map/all_to_all | solution.py:32
  1592.7 147.2 %scatter_custom_fusion.3 = f32[4096,1024]{1,0:T(8,128)} fusion(f32[4096,1024]{1,0:T(8,128)} %convert_element_type.20, s32[16384]{0:T(1024)} %bitcast.92, bf16[16384,1024]{1,0:T(8,128)(2,1)} %bitcast.50), kind=kCustom, calls=%fused_computation.16 | custom fusion | flops 33554432 | bytes 50331648 | tf_op jit(solution)/shard_map/scatter-add | solution.py:33
  1739.9 9.1 convert_element_type.25
  (13 shorter events, 0.1 us)
Async XLA Ops:
  154.2 84.8 %copy-start = (s32[32,1,512]{2,1,0:T(1,128)}, s32[32,1,512]{2,1,0:T(1,128)S(1)}, u32[]{:S(2)}) copy-start(s32[32,1,512]{2,1,0:T(1,128)S(1)} %all_to_all.19) | copy-start | bytes 196612
  261.9 462.0 %all-to-all-start.1 = ((bf16[32,512,1024]{2,1,0:T(8,128)(2,1)}), bf16[32,512,1024]{2,1,0:T(8,128)(2,1)}, u32[]{:S(2)}, u32[]{:S(2)}) async-start(bf16[32,512,1024]{2,1,0:T(8,128)(2,1)} %broadcast_select_fusion), calls=%async_computation.1 | async-start | bytes 67108864 | tf_op jit(solution)/shard_map/all_to_all | solution.py:26
  723.9 150.1 %copy-start.1 = (pred[8192]{0:T(1024)(128)(4,1)S(1)}, pred[8192]{0:T(1024)(128)(4,1)}, u32[]{:S(2)}) copy-start(pred[8192]{0:T(1024)(128)(4,1)} %get-tuple-element.36) | copy-start | bytes 24580
  874.1 73.6 %copy-start.2 = (f32[1,8192]{1,0:T(1,128)S(1)}, f32[1,8192]{1,0:T(1,128)}, u32[]{:S(2)}) copy-start(f32[1,8192]{1,0:T(1,128)} %param.7) | copy-start | bytes 98308
  1134.4 458.2 %all-to-all-start.2 = ((bf16[32,512,1024]{2,1,0:T(8,128)(2,1)}), bf16[32,512,1024]{2,1,0:T(8,128)(2,1)}, u32[]{:S(2)}, u32[]{:S(2)}) async-start(bf16[32,512,1024]{2,1,0:T(8,128)(2,1)} %bitcast.90), calls=%async_computation.2 | async-start | bytes 67108864 | tf_op jit(solution)/shard_map/all_to_all | solution.py:32
where the time goes:
time: 1760 us; the launch traced here: 1750 us
  waiting for transfers between devices  891 us (51%)
  local copies, waits for them, and re-layouts  399 us (23%)
  other arithmetic  294 us (17%)
  matrix products  129 us (7%)
  blocking collectives  25.6 us (1%)
    all_to_all x1, waiting for transfers between devices, local_layer(): lax.all_to_all(send_rows, 'ep', 0, 0, tiled=True)  448 us
    all_to_all x1, waiting for transfers between devices, local_layer(): lax.all_to_all(back_rows.reshape(group_size, pair_cap, model_width), 'ep'...  442 us
    gather x1, local copies, waits for them, and re-layouts, local_layer(): jnp.take(received, slot_idx, axis=0).reshape(exp_loc, cap_rows, model_width)  150 us
    scatter-add x1, other arithmetic, local_layer(): jax.ops.segment_sum(returned.astype(jnp.float32), wanted, num_segments=to...  147 us
    scatter x2, local copies, waits for them, and re-layouts, local_layer(): jnp.zeros((group_size * pair_cap, model_width), jnp.bfloat16).at[slot_idx]  132 us
    gather x1, local copies, waits for them, and re-layouts, local_layer(): jnp.take(x_loc, wanted, axis=0).reshape(group_size, pair_cap, model_width)  84.7 us
    dot_general x1, matrix products, local_layer(): jnp.einsum('ecd,edf->ecf', picked, up_loc, preferred_element_type=jnp.flo...  73.6 us
    scatter-add x1, other arithmetic, local_layer(): counts = jnp.bincount(src_dev, length=group_size)  57 us
  transfers between devices with their start and end apart: 2, of which 2 were waited for; matrix products, arithmetic and copies ran while one was open for 1% of the time, Pallas kernels for 0%

commit v1 on v0

v1 whole, which is shorter than its diff:
```python
import jax
import jax.numpy as jnp
from jax import lax
from jax.sharding import PartitionSpec as P

CHUNKS = 4


def solution(mesh):
    group_size = mesh.shape["ep"]

    def local_layer(x_loc, sel_loc, gate_loc, up_loc, down_loc):
        tok_loc, model_width = x_loc.shape
        entry_count = sel_loc.shape[0] * sel_loc.shape[1]
        pair_cap = 2 * entry_count // group_size
        part = pair_cap // CHUNKS
        sel = sel_loc.reshape(entry_count)
        dev_ids = jnp.arange(group_size, dtype=jnp.int32)
        src_dev = sel // tok_loc
        counts = jnp.sum((src_dev[:, None] == dev_ids[None, :]).astype(jnp.int32), axis=0)
        lower = dev_ids[:, None] >= dev_ids[None, :]
        free_end = jnp.sum(jnp.where(lower, (pair_cap - counts)[None, :], 0), axis=1)
        fill_ids = jnp.arange(group_size * pair_cap - entry_count, dtype=jnp.int32)
        fill_dev = jnp.sum((free_end[None, :] <= fill_ids[:, None]).astype(jnp.int32), axis=1)
        keys = jnp.concatenate([sel + src_dev * tok_loc, fill_dev * (2 * tok_loc) + tok_loc])
        gates = jnp.concatenate([gate_loc.reshape(entry_count), jnp.zeros(fill_ids.shape, jnp.float32)])
        keys, gates = lax.sort((keys, gates), num_keys=1, is_stable=False)
        request = keys.reshape(group_size, pair_cap) - dev_ids[:, None] * (2 * tok_loc)
        gates = gates.reshape(group_size, pair_cap)
        wanted = lax.all_to_all(request, "ep", 0, 0, tiled=True)

        rows = group_size * part
        acc = x_loc.astype(jnp.float32)
        sent = []
        for k in range(CHUNKS):
            idx = wanted[:, k * part:(k + 1) * part].reshape(rows)
            send = x_loc.at[jnp.minimum(idx, tok_loc - 1)].get(mode="promise_in_bounds")
            sent.append((idx, lax.all_to_all(send.reshape(group_size, part, model_width), "ep", 0, 0, tiled=True)))
        back = []
        for k in range(CHUNKS):
            idx, got = sent[k]
            hidden = jax.nn.gelu(jnp.dot(got.reshape(rows, model_width), up_loc[0], preferred_element_type=jnp.float32), approximate=True).astype(jnp.bfloat16)
            out = jnp.dot(hidden, down_loc[0], preferred_element_type=jnp.float32)
            gate = gates[:, k * part:(k + 1) * part].reshape(rows, 1)
            contrib = (out * gate).astype(jnp.bfloat16).reshape(group_size, part, model_width)
            back.append((idx, lax.all_to_all(contrib, "ep", 0, 0, tiled=True)))
        for idx, ret in back:
            acc = acc.at[idx].add(ret.reshape(rows, model_width).astype(jnp.float32), mode="drop")
        return acc.astype(jnp.bfloat16)

    row_spec = P(("dp", "ep"), None)
    weight_spec = P("ep", None, None)
    return jax.shard_map(local_layer, mesh=mesh, in_specs=(row_spec, row_spec, row_spec, weight_spec, weight_spec), out_specs=row_spec, check_vma=False)
```

time: 1760 us -> 1090 us (0.62)
  waiting for transfers between devices: 891 us -> 432 us
  local copies, waits for them, and re-layouts: 399 us -> 103 us
  matrix products: 129 us -> 271 us
  other arithmetic: 294 us -> 216 us
  starting transfers between devices: 11.1 us -> 40.7 us
    all_to_all x2 -> x8, waiting for transfers between devices: 891 us -> 432 us  [the longest x4 299 us: local_layer(): lax.all_to_all(send.reshape(group_size, part, model_width), 'ep', 0, 0, t...]
    scatter x3 -> x0, local copies, waits for them, and re-layouts: 162 us -> none  [the longest x2 132 us: local_layer(): jnp.zeros((group_size * pair_cap, model_width), jnp.bfloat16).at[slot_idx]]
    dot_general x2 -> x8, matrix products: 129 us -> 271 us  [the longest x4 155 us: local_layer(): jnp.dot(got.reshape(rows, model_width), up_loc[0], preferred_element_type...]
    gather x4, local copies, waits for them, and re-layouts: 236 us -> 101 us  [local_layer(): send = x_loc.at[jnp.minimum(idx, tok_loc - 1)].get(mode='promise_in_bounds')]
    all_to_all x2 -> x8, starting transfers between devices: 11.1 us -> 40.7 us  [the longest x4 21.5 us: local_layer(): lax.all_to_all(send.reshape(group_size, part, model_width), 'ep', 0, 0, t...]
    select_n x2 -> x4, other arithmetic: 22.9 us -> 2.55 us  [local_layer(): send = x_loc.at[jnp.minimum(idx, tok_loc - 1)].get(mode='promise_in_bounds')]
    scatter-add x2 -> x4, other arithmetic: 204 us -> 186 us  [local_layer(): acc.at[idx]]
  transfers between devices with their start and end apart: 2 -> 8, of which waited for: 2 -> 7; matrix products, arithmetic and copies ran while one was open for 1% -> 46% of each run, Pallas kernels for 0% -> 0%
where the time goes in v1:
time: 1090 us; the launch traced here: 1080 us
  waiting for transfers between devices  432 us (40%)
  matrix products  271 us (25%)
  other arithmetic  216 us (20%)
  local copies, waits for them, and re-layouts  103 us (9%)
  starting transfers between devices  40.7 us (4%)
  blocking collectives  12.9 us (1%)
    all_to_all x4, waiting for transfers between devices, local_layer(): lax.all_to_all(send.reshape(group_size, part, model_width), 'ep', 0, 0, t...  299 us
    scatter-add x4, other arithmetic, local_layer(): acc.at[idx]  186 us
    dot_general x4, matrix products, local_layer(): jnp.dot(got.reshape(rows, model_width), up_loc[0], preferred_element_type...  155 us
    all_to_all x4, waiting for transfers between devices, local_layer(): back.append((idx, lax.all_to_all(contrib, 'ep', 0, 0, tiled=True)))  133 us
    dot_general x4, matrix products, local_layer(): out = jnp.dot(hidden, down_loc[0], preferred_element_type=jnp.float32)  116 us
    gather x4, local copies, waits for them, and re-layouts, local_layer(): send = x_loc.at[jnp.minimum(idx, tok_loc - 1)].get(mode='promise_in_bounds')  101 us
  transfers between devices with their start and end apart: 8, of which 7 were waited for; matrix products, arithmetic and copies ran while one was open for 46% of the time, Pallas kernels for 0%

profile of v1, /device:TPU:107, one launch (start us, length us, event | category | flops | bytes accessed | tf_op | source)
XLA Modules:
  0.0 1076.6 jit_solution(2111115755095503437)
XLA Ops:
  2.2 6.4 sort.15
  8.7 12.9 %all_to_all.49 = s32[32,1,512]{2,1,0:T(1,128)S(1)} all-to-all(s32[32,1,512]{2,1,0:T(1,128)S(1)} %broadcast_subtract_fusion), channel_id=1, replica_groups=mesh['dp'=1,'ep'=32] {'ep'}, dimensions={0} | all-to-all | bytes 131072 | tf_op jit(solution)/shard_map/all_to_all | solution.py:30
  22.3 25.2 %gather_fusion = bf16[4096,1024]{1,0:T(8,128)(2,1)} fusion(bf16[4096,1024]{1,0:T(8,128)(2,1)} %param.5, s32[4096]{0:T(1024)S(1)} %broadcast_clamp_fusion.3), kind=kCustom, calls=%fused_computation | custom fusion | bytes 16793600 | tf_op jit(solution)/shard_map/gather | solution.py:37
  47.6 5.8 all-to-all-start.1
  54.0 25.3 %gather_fusion.1 = bf16[4096,1024]{1,0:T(8,128)(2,1)} fusion(bf16[4096,1024]{1,0:T(8,128)(2,1)} %param.5, s32[4096]{0:T(1024)S(1)} %broadcast_clamp_fusion.2), kind=kCustom, calls=%fused_computation.1 | custom fusion | bytes 16793600 | tf_op jit(solution)/shard_map/gather | solution.py:37
  79.3 86.2 %all-to-all-done.1 = bf16[32,128,1024]{2,1,0:T(8,128)(2,1)} async-done(((bf16[32,128,1024]{2,1,0:T(8,128)(2,1)}), bf16[32,128,1024]{2,1,0:T(8,128)(2,1)}, u32[]{:S(2)}, u32[]{:S(2)}) %all-to-all-start.1) | async-done | bytes 8388640 | tf_op jit(solution)/shard_map/all_to_all | solution.py:38
  170.5 25.2 %gather_fusion.2 = bf16[4096,1024]{1,0:T(8,128)(2,1)} fusion(bf16[4096,1024]{1,0:T(8,128)(2,1)} %param.5, s32[4096]{0:T(1024)S(1)} %broadcast_clamp_fusion.1), kind=kCustom, calls=%fused_computation.2 | custom fusion | bytes 16793600 | tf_op jit(solution)/shard_map/gather | solution.py:37
  195.7 85.9 %all-to-all-done.3 = bf16[32,128,1024]{2,1,0:T(8,128)(2,1)} async-done(((bf16[32,128,1024]{2,1,0:T(8,128)(2,1)}), bf16[32,128,1024]{2,1,0:T(8,128)(2,1)}, u32[]{:S(2)}, u32[]{:S(2)}) %all-to-all-start.3) | async-done | bytes 8388640 | tf_op jit(solution)/shard_map/all_to_all | solution.py:38
  281.7 5.5 all-to-all-start.5
  288.5 25.3 %gather_fusion.3 = bf16[4096,1024]{1,0:T(8,128)(2,1)} fusion(bf16[4096,1024]{1,0:T(8,128)(2,1)} %param.5, s32[4096]{0:T(1024)S(1)} %broadcast_clamp_fusion), kind=kCustom, calls=%fused_computation.3 | custom fusion | bytes 16793600 | tf_op jit(solution)/shard_map/gather | solution.py:37
  313.8 84.0 %all-to-all-done.5 = bf16[32,128,1024]{2,1,0:T(8,128)(2,1)} async-done(((bf16[32,128,1024]{2,1,0:T(8,128)(2,1)}), bf16[32,128,1024]{2,1,0:T(8,128)(2,1)}, u32[]{:S(2)}, u32[]{:S(2)}) %all-to-all-start.5) | async-done | bytes 8388640 | tf_op jit(solution)/shard_map/all_to_all | solution.py:38
  397.9 5.9 all-to-all-start.7
  403.8 38.6 %fusion.7.clone.2 = bf16[4096,2816]{1,0:T(8,128)(2,1)} fusion(bf16[4096,1024]{1,0:T(8,128)(2,1)} %bitcast.7, bf16[1,1024,2816]{2,1,0:T(8,128)(2,1)} %param.8), kind=kOutput, calls=%fused_computation.19.clone.clone.clone | convolution fusion | flops 23726129152 | bytes 37224448 | tf_op jit(solution)/shard_map/dot_general | solution.py:42
  442.3 30.3 %multiply_convert_fusion.3 = bf16[4096,1024]{1,0:T(8,128)(2,1)} fusion(f32[4096]{0:T(1024)S(1)} %get-tuple-element.12, bf16[1,2816,1024]{2,1,0:T(8,128)(2,1)} %param.9, bf16[4096,2816]{1,0:T(8,128)(2,1)} %fusion.7.clone.2), kind=kOutput, calls=%fused_computation.55 | convolution fusion | flops 23630708736 | bytes 37240832 | tf_op jit(solution)/shard_map/dot_general | solution.py:43
  472.6 43.0 %all-to-all-done.7 = bf16[32,128,1024]{2,1,0:T(8,128)(2,1)} async-done(((bf16[32,128,1024]{2,1,0:T(8,128)(2,1)}), bf16[32,128,1024]{2,1,0:T(8,128)(2,1)}, u32[]{:S(2)}, u32[]{:S(2)}) %all-to-all-start.7) | async-done | bytes 8388640 | tf_op jit(solution)/shard_map/all_to_all | solution.py:38
  520.2 38.7 %fusion.15.clone.2 = bf16[4096,2816]{1,0:T(8,128)(2,1)} fusion(bf16[4096,1024]{1,0:T(8,128)(2,1)} %bitcast.17, bf16[1,1024,2816]{2,1,0:T(8,128)(2,1)} %param.8), kind=kOutput, calls=%fused_computation.27.clone.clone.clone | convolution fusion | flops 23726129152 | bytes 37224448 | tf_op jit(solution)/shard_map/dot_general | solution.py:42
  559.0 28.9 %multiply_convert_fusion.2 = bf16[4096,1024]{1,0:T(8,128)(2,1)} fusion(f32[4096]{0:T(1024)S(1)} %copy-done.2, bf16[1,2816,1024]{2,1,0:T(8,128)(2,1)S(1)} %bitcast.114, bf16[4096,2816]{1,0:T(8,128)(2,1)} %fusion.15.clone.2), kind=kOutput, calls=%fused_computation.54 | convolution fusion | flops 23630708736 | bytes 37240832 | tf_op jit(solution)/shard_map/dot_general | solution.py:43
  587.9 44.2 %all-to-all-done.2 = bf16[32,128,1024]{2,1,0:T(8,128)(2,1)} async-done(((bf16[32,128,1024]{2,1,0:T(8,128)(2,1)}), bf16[32,128,1024]{2,1,0:T(8,128)(2,1)}, u32[]{:S(2)}, u32[]{:S(2)}) %all-to-all-start.2) | async-done | bytes 8388640 | tf_op jit(solution)/shard_map/all_to_all | solution.py:46
  632.0 5.0 all-to-all-start.4
  637.0 38.7 %fusion.23.clone.2 = bf16[4096,2816]{1,0:T(8,128)(2,1)} fusion(bf16[4096,1024]{1,0:T(8,128)(2,1)} %bitcast.25, bf16[1,1024,2816]{2,1,0:T(8,128)(2,1)} %param.8), kind=kOutput, calls=%fused_computation.35.clone.clone.clone | convolution fusion | flops 23726129152 | bytes 37224448 | tf_op jit(solution)/shard_map/dot_general | solution.py:42
  675.8 28.6 %multiply_convert_fusion.1 = bf16[4096,1024]{1,0:T(8,128)(2,1)} fusion(f32[4096]{0:T(1024)S(1)} %copy-done.1, bf16[1,2816,1024]{2,1,0:T(8,128)(2,1)S(1)} %bitcast.116, bf16[4096,2816]{1,0:T(8,128)(2,1)} %fusion.23.clone.2), kind=kOutput, calls=%fused_computation.53 | convolution fusion | flops 23630708736 | bytes 37240832 | tf_op jit(solution)/shard_map/dot_general | solution.py:43
  704.4 44.5 %all-to-all-done.4 = bf16[32,128,1024]{2,1,0:T(8,128)(2,1)} async-done(((bf16[32,128,1024]{2,1,0:T(8,128)(2,1)}), bf16[32,128,1024]{2,1,0:T(8,128)(2,1)}, u32[]{:S(2)}, u32[]{:S(2)}) %all-to-all-start.4) | async-done | bytes 8388640 | tf_op jit(solution)/shard_map/all_to_all | solution.py:46
  748.8 5.0 all-to-all-start.6
  753.9 38.7 %fusion.31.clone.4 = bf16[4096,2816]{1,0:T(8,128)(2,1)} fusion(bf16[4096,1024]{1,0:T(8,128)(2,1)} %bitcast.33, bf16[1,1024,2816]{2,1,0:T(8,128)(2,1)} %param.8), kind=kOutput, calls=%fused_computation.43.clone.clone.clone.1 | convolution fusion | flops 23726129152 | bytes 37224448 | tf_op jit(solution)/shard_map/dot_general | solution.py:42
  792.6 28.7 %multiply_convert_fusion = bf16[4096,1024]{1,0:T(8,128)(2,1)} fusion(f32[4096]{0:T(1024)S(1)} %copy-done, bf16[1,2816,1024]{2,1,0:T(8,128)(2,1)S(1)} %bitcast.118, bf16[4096,2816]{1,0:T(8,128)(2,1)} %fusion.31.clone.4), kind=kOutput, calls=%fused_computation.52 | convolution fusion | flops 23630708736 | bytes 37240832 | tf_op jit(solution)/shard_map/dot_general | solution.py:43
  821.2 44.4 %all-to-all-done.6 = bf16[32,128,1024]{2,1,0:T(8,128)(2,1)} async-done(((bf16[32,128,1024]{2,1,0:T(8,128)(2,1)}), bf16[32,128,1024]{2,1,0:T(8,128)(2,1)}, u32[]{:S(2)}, u32[]{:S(2)}) %all-to-all-start.6) | async-done | bytes 8388640 | tf_op jit(solution)/shard_map/all_to_all | solution.py:46
  870.3 11.3 %convert_element_type.60 = f32[4096,1024]{1,0:T(8,128)} convert(bf16[4096,1024]{1,0:T(8,128)(2,1)} %param.5) | non-fusion elementwise | flops 4194304 | bytes 25165824 | tf_op jit(solution)/shard_map/convert_element_type | solution.py:33
  881.6 46.3 %scatter_custom_fusion = f32[4096,1024]{1,0:T(8,128)} fusion(f32[4096,1024]{1,0:T(8,128)} %convert_element_type.60, s32[4096]{0:T(1024)} %bitcast.109, bf16[4096,1024]{1,0:T(8,128)(2,1)} %bitcast.37), kind=kCustom, calls=%fused_computation.50 | custom fusion | flops 8388608 | bytes 25165824 | tf_op jit(solution)/shard_map/scatter-add | solution.py:48
  927.9 46.6 %scatter_custom_fusion.1 = f32[4096,1024]{1,0:T(8,128)} fusion(f32[4096,1024]{1,0:T(8,128)} %scatter_custom_fusion, s32[4096]{0:T(1024)} %bitcast.110, bf16[4096,1024]{1,0:T(8,128)(2,1)} %bitcast.38), kind=kCustom, calls=%fused_computation.48 | custom fusion | flops 8388608 | bytes 25165824 | tf_op jit(solution)/shard_map/scatter-add | solution.py:48
  974.4 46.3 %scatter_custom_fusion.2 = f32[4096,1024]{1,0:T(8,128)} fusion(f32[4096,1024]{1,0:T(8,128)} %scatter_custom_fusion.1, s32[4096]{0:T(1024)} %bitcast.111, bf16[4096,1024]{1,0:T(8,128)(2,1)} %bitcast.39), kind=kCustom, calls=%fused_computation.46 | custom fusion | flops 8388608 | bytes 25165824 | tf_op jit(solution)/shard_map/scatter-add | solution.py:48
  1020.8 46.3 %scatter_custom_fusion.3 = f32[4096,1024]{1,0:T(8,128)} fusion(f32[4096,1024]{1,0:T(8,128)} %scatter_custom_fusion.2, s32[4096]{0:T(1024)} %bitcast.112, bf16[4096,1024]{1,0:T(8,128)(2,1)} %bitcast.40), kind=kCustom, calls=%fused_computation.44 | custom fusion | flops 8388608 | bytes 25165824 | tf_op jit(solution)/shard_map/scatter-add | solution.py:48
  1067.1 9.1 convert_element_type.79
  (47 shorter events, 19.1 us)
Async XLA Ops:
  47.6 117.9 %all-to-all-start.1 = ((bf16[32,128,1024]{2,1,0:T(8,128)(2,1)}), bf16[32,128,1024]{2,1,0:T(8,128)(2,1)}, u32[]{:S(2)}, u32[]{:S(2)}) async-start(bf16[32,128,1024]{2,1,0:T(8,128)(2,1)} %bitcast.92), calls=%async_computation.1 | async-start | bytes 16777216 | tf_op jit(solution)/shard_map/all_to_all | solution.py:38
  165.5 116.2 %all-to-all-start.3 = ((bf16[32,128,1024]{2,1,0:T(8,128)(2,1)}), bf16[32,128,1024]{2,1,0:T(8,128)(2,1)}, u32[]{:S(2)}, u32[]{:S(2)}) async-start(bf16[32,128,1024]{2,1,0:T(8,128)(2,1)} %bitcast.90), calls=%async_computation.3 | async-start | bytes 16777216 | tf_op jit(solution)/shard_map/all_to_all | solution.py:38
  281.7 116.2 %all-to-all-start.5 = ((bf16[32,128,1024]{2,1,0:T(8,128)(2,1)}), bf16[32,128,1024]{2,1,0:T(8,128)(2,1)}, u32[]{:S(2)}, u32[]{:S(2)}) async-start(bf16[32,128,1024]{2,1,0:T(8,128)(2,1)} %bitcast.89), calls=%async_computation.5 | async-start | bytes 16777216 | tf_op jit(solution)/shard_map/all_to_all | solution.py:38
  397.9 117.7 %all-to-all-start.7 = ((bf16[32,128,1024]{2,1,0:T(8,128)(2,1)}), bf16[32,128,1024]{2,1,0:T(8,128)(2,1)}, u32[]{:S(2)}, u32[]{:S(2)}) async-start(bf16[32,128,1024]{2,1,0:T(8,128)(2,1)} %bitcast.91), calls=%async_computation.7 | async-start | bytes 16777216 | tf_op jit(solution)/shard_map/all_to_all | solution.py:38
  515.6 43.4 %slice-start = ((s8[5767168]{0:T(1024)(128)(4,1)}), s8[1572864]{0:T(1024)(128)(4,1)S(1)}, s32[]{:S(2)}) async-start(s8[5767168]{0:T(1024)(128)(4,1)} %bitcast.113), calls=%async_computation.9 | async-start | bytes 3145728
  515.6 116.4 %all-to-all-start.2 = ((bf16[32,128,1024]{2,1,0:T(8,128)(2,1)}), bf16[32,128,1024]{2,1,0:T(8,128)(2,1)}, u32[]{:S(2)}, u32[]{:S(2)}) async-start(bf16[32,128,1024]{2,1,0:T(8,128)(2,1)} %bitcast.95), calls=%async_computation.2 | async-start | bytes 16777216 | tf_op jit(solution)/shard_map/all_to_all | solution.py:46
  520.2 38.7 %copy-start.2 = (f32[4096]{0:T(1024)S(1)}, f32[4096]{0:T(1024)}, u32[]{:S(2)}) copy-start(f32[4096]{0:T(1024)} %get-tuple-element.11) | copy-start | bytes 49156
  520.2 38.7 %slice-start.1 = ((s8[5767168]{0:T(1024)(128)(4,1)}), s8[4194304]{0:T(1024)(128)(4,1)S(1)}, s32[]{:S(2)}) async-start(s8[5767168]{0:T(1024)(128)(4,1)} %bitcast.113), calls=%async_computation.10 | async-start | bytes 8388608
  632.0 43.7 %slice-start.2 = ((s8[5767168]{0:T(1024)(128)(4,1)}), s8[1572864]{0:T(1024)(128)(4,1)S(1)}, s32[]{:S(2)}) async-start(s8[5767168]{0:T(1024)(128)(4,1)} %bitcast.115), calls=%async_computation.11 | async-start | bytes 3145728
  632.0 116.8 %all-to-all-start.4 = ((bf16[32,128,1024]{2,1,0:T(8,128)(2,1)}), bf16[32,128,1024]{2,1,0:T(8,128)(2,1)}, u32[]{:S(2)}, u32[]{:S(2)}) async-start(bf16[32,128,1024]{2,1,0:T(8,128)(2,1)} %bitcast.96), calls=%async_computation.4 | async-start | bytes 16777216 | tf_op jit(solution)/shard_map/all_to_all | solution.py:46
  637.0 38.7 %copy-start.1 = (f32[4096]{0:T(1024)S(1)}, f32[4096]{0:T(1024)}, u32[]{:S(2)}) copy-start(f32[4096]{0:T(1024)} %get-tuple-element.10) | copy-start | bytes 49156
  637.0 38.7 %slice-start.3 = ((s8[5767168]{0:T(1024)(128)(4,1)}), s8[4194304]{0:T(1024)(128)(4,1)S(1)}, s32[]{:S(2)}) async-start(s8[5767168]{0:T(1024)(128)(4,1)} %bitcast.115), calls=%async_computation.12 | async-start | bytes 8388608
  748.8 43.7 %slice-start.4 = ((s8[5767168]{0:T(1024)(128)(4,1)}), s8[1572864]{0:T(1024)(128)(4,1)S(1)}, s32[]{:S(2)}) async-start(s8[5767168]{0:T(1024)(128)(4,1)} %bitcast.117), calls=%async_computation.13 | async-start | bytes 3145728
  748.8 116.8 %all-to-all-start.6 = ((bf16[32,128,1024]{2,1,0:T(8,128)(2,1)}), bf16[32,128,1024]{2,1,0:T(8,128)(2,1)}, u32[]{:S(2)}, u32[]{:S(2)}) async-start(bf16[32,128,1024]{2,1,0:T(8,128)(2,1)} %bitcast.94), calls=%async_computation.6 | async-start | bytes 16777216 | tf_op jit(solution)/shard_map/all_to_all | solution.py:46
  753.8 38.7 %copy-start = (f32[4096]{0:T(1024)S(1)}, f32[4096]{0:T(1024)}, u32[]{:S(2)}) copy-start(f32[4096]{0:T(1024)} %get-tuple-element.9) | copy-start | bytes 49156
  753.8 38.7 %slice-start.5 = ((s8[5767168]{0:T(1024)(128)(4,1)}), s8[4194304]{0:T(1024)(128)(4,1)S(1)}, s32[]{:S(2)}) async-start(s8[5767168]{0:T(1024)(128)(4,1)} %bitcast.117), calls=%async_computation.14 | async-start | bytes 8388608
  865.7 155.1 %all-to-all-start.8 = ((bf16[32,128,1024]{2,1,0:T(8,128)(2,1)}), bf16[32,128,1024]{2,1,0:T(8,128)(2,1)}, u32[]{:S(2)}, u32[]{:S(2)}) async-start(bf16[32,128,1024]{2,1,0:T(8,128)(2,1)} %bitcast.93), calls=%async_computation.8 | async-start | bytes 16777216 | tf_op jit(solution)/shard_map/all_to_all | solution.py:46

commit v2 on v1

--- a/solution.py
+++ b/solution.py
@@ -1,9 +1,94 @@
+import functools
+
 import jax
 import jax.numpy as jnp
 from jax import lax
+from jax.experimental import pallas as pl
+from jax.experimental.pallas import tpu as pltpu
 from jax.sharding import PartitionSpec as P
 
-CHUNKS = 4
+CHUNKS = 2
+LANES = 128
+BATCH = 8
+VMEM_LIMIT = 60 * 1024 * 1024
+
+
+def pack_kernel(idx_ref, x_ref, out_ref):
+    rows = out_ref.shape[0]
+    base = pl.program_id(0) * rows
+
+    def body(b, _):
+        vals = [x_ref[idx_ref[base + b * BATCH + j]] for j in range(BATCH)]
+        for j in range(BATCH):
+            out_ref[b * BATCH + j] = vals[j]
+        return 0
+
+    lax.fori_loop(0, rows // BATCH, body, 0)
+
+
+def pack_rows(x3, idx, block):
+    rows = idx.shape[0]
+    tail = x3.shape[1:]
+    return pl.pallas_call(
+        pack_kernel,
+        grid_spec=pltpu.PrefetchScalarGridSpec(
+            num_scalar_prefetch=1,
+            grid=(rows // block,),
+            in_specs=[pl.BlockSpec(x3.shape, lambda i, idx: (0, 0, 0))],
+            out_specs=pl.BlockSpec((block,) + tail, lambda i, idx: (i, 0, 0)),
+        ),
+        out_shape=jax.ShapeDtypeStruct((rows,) + tail, x3.dtype),
+        compiler_params=pltpu.CompilerParams(vmem_limit_bytes=VMEM_LIMIT),
+        cost_estimate=pl.CostEstimate(flops=rows * 4096, bytes_accessed=rows * 4096, transcendentals=0),
+    )(idx, x3)
+
+
+def combine_kernel(idx_ref, cnt_ref, base_ref, ret_ref, out_ref, acc, sem):
+    g = pl.program_id(0)
+    part = ret_ref.shape[0]
+    tok = base_ref.shape[0]
+
+    @pl.when(g == 0)
+    def _():
+        load = pltpu.make_async_copy(base_ref, acc.at[pl.ds(0, tok)], sem)
+        load.start()
+        load.wait()
+
+    def body(b, _):
+        at = [idx_ref[g * part + b * BATCH + j] for j in range(BATCH)]
+        sums = [acc[at[j]] + ret_ref[b * BATCH + j].astype(jnp.float32) for j in range(BATCH)]
+        for j in range(BATCH):
+            acc[at[j]] = sums[j]
+        return 0
+
+    lax.fori_loop(0, (cnt_ref[g] + BATCH - 1) // BATCH, body, 0)
+
+    @pl.when(g == pl.num_programs(0) - 1)
+    def _():
+        store = pltpu.make_async_copy(acc.at[pl.ds(0, tok)], out_ref, sem)
+        store.start()
+        store.wait()
+
+
+def combine_rows(base, ret, idx, cnt):
+    group, part = ret.shape[:2]
+    tail = base.shape[1:]
+    return pl.pallas_call(
+        combine_kernel,
+        grid_spec=pltpu.PrefetchScalarGridSpec(
+            num_scalar_prefetch=2,
+            grid=(group,),
+            in_specs=[
+                pl.BlockSpec(memory_space=pl.ANY),
+                pl.BlockSpec((None, part) + tail, lambda g, idx, cnt: (g, 0, 0, 0)),
+            ],
+            out_specs=pl.BlockSpec(memory_space=pl.ANY),
+            scratch_shapes=[pltpu.VMEM((base.shape[0] + 8,) + tail, jnp.float32), pltpu.SemaphoreType.DMA],
+        ),
+        out_shape=jax.ShapeDtypeStruct(base.shape, jnp.float32),
+        compiler_params=pltpu.CompilerParams(vmem_limit_bytes=VMEM_LIMIT),
+        cost_estimate=pl.CostEstimate(flops=group * part * 4096, bytes_accessed=group * part * 6144, transcendentals=0),
+    )(idx, cnt, base, ret)
 
 
 def solution(mesh):
@@ -11,6 +96,7 @@
 
     def local_layer(x_loc, sel_loc, gate_loc, up_loc, down_loc):
         tok_loc, model_width = x_loc.shape
+        tail = (model_width // LANES, LANES)
         entry_count = sel_loc.shape[0] * sel_loc.shape[1]
         pair_cap = 2 * entry_count // group_size
         part = pair_cap // CHUNKS
@@ -28,25 +114,27 @@
         request = keys.reshape(group_size, pair_cap) - dev_ids[:, None] * (2 * tok_loc)
         gates = gates.reshape(group_size, pair_cap)
         wanted = lax.all_to_all(request, "ep", 0, 0, tiled=True)
+        filled = jnp.sum((wanted < tok_loc).astype(jnp.int32), axis=1)
 
         rows = group_size * part
-        acc = x_loc.astype(jnp.float32)
+        x3 = x_loc.reshape((tok_loc,) + tail)
         sent = []
         for k in range(CHUNKS):
             idx = wanted[:, k * part:(k + 1) * part].reshape(rows)
-            send = x_loc.at[jnp.minimum(idx, tok_loc - 1)].get(mode="promise_in_bounds")
-            sent.append((idx, lax.all_to_all(send.reshape(group_size, part, model_width), "ep", 0, 0, tiled=True)))
+            send = pack_rows(x3, jnp.minimum(idx, tok_loc - 1), rows // 8)
+            sent.append((idx, lax.all_to_all(send.reshape((group_size, part) + tail), "ep", 0, 0, tiled=True)))
         back = []
         for k in range(CHUNKS):
             idx, got = sent[k]
             hidden = jax.nn.gelu(jnp.dot(got.reshape(rows, model_width), up_loc[0], preferred_element_type=jnp.float32), approximate=True).astype(jnp.bfloat16)
             out = jnp.dot(hidden, down_loc[0], preferred_element_type=jnp.float32)
             gate = gates[:, k * part:(k + 1) * part].reshape(rows, 1)
-            contrib = (out * gate).astype(jnp.bfloat16).reshape(group_size, part, model_width)
+            contrib = (out * gate).astype(jnp.bfloat16).reshape((group_size, part) + tail)
             back.append((idx, lax.all_to_all(contrib, "ep", 0, 0, tiled=True)))
-        for idx, ret in back:
-            acc = acc.at[idx].add(ret.reshape(rows, model_width).astype(jnp.float32), mode="drop")
-        return acc.astype(jnp.bfloat16)
+        acc = x3.astype(jnp.float32)
+        for k, (idx, ret) in enumerate(back):
+            acc = combine_rows(acc, ret, idx, jnp.clip(filled - k * part, 0, part))
+        return acc.reshape(tok_loc, model_width).astype(jnp.bfloat16)
 
     row_spec = P(("dp", "ep"), None)
     weight_spec = P("ep", None, None)

time: 1090 us -> 1020 us (0.936)
  other arithmetic: 216 us -> 28.8 us
  waiting for transfers between devices: 432 us -> 551 us
  Pallas kernels: 0 us -> 111 us
  local copies, waits for them, and re-layouts: 103 us -> 38.6 us
  matrix products: 271 us -> 256 us
  blocking collectives: 12.9 us -> 0 us
  starting transfers between devices: 40.7 us -> 28 us
    scatter-add x4 -> x0, other arithmetic: 186 us -> none  [local_layer(): acc.at[idx]]
    all_to_all x4 -> x2, waiting for transfers between devices: 133 us -> 263 us  [local_layer(): back.append((idx, lax.all_to_all(contrib, 'ep', 0, 0, tiled=True)))]
    pallas_call x0 -> x4, Pallas kernels: none -> 111 us  [the longest x2 69.1 us: combine_rows(): pl.pallas_call(combine_kernel, grid_spec=pltpu.PrefetchScalarGridSpec(num...]
    gather x4 -> x0, local copies, waits for them, and re-layouts: 101 us -> none  [local_layer(): send = x_loc.at[jnp.minimum(idx, tok_loc - 1)].get(mode='promise_in_bounds')]
    unnamed x19 -> x21, local copies, waits for them, and re-layouts: 0.05 us -> 37.8 us
    all_to_all x1 -> x0, blocking collectives: 12.9 us -> none  [local_layer(): wanted = lax.all_to_all(request, 'ep', 0, 0, tiled=True)]
    all_to_all x4 -> x3, waiting for transfers between devices: 299 us -> 288 us  [the longest x2 288 us: local_layer(): lax.all_to_all(send.reshape((group_size, part) + tail), 'ep', 0, 0, tiled...]
    dot_general x4 -> x2, matrix products: 155 us -> 146 us  [local_layer(): jnp.dot(got.reshape(rows, model_width), up_loc[0], preferred_element_type...]
  transfers between devices with their start and end apart: 8 -> 5, of which waited for: 7 -> 4; matrix products, arithmetic and copies ran while one was open for 46% -> 29% of each run, Pallas kernels for 0% -> 6%
where the time goes in v2:
time: 1020 us; the launch traced here: 1010 us
  waiting for transfers between devices  551 us (54%)
  matrix products  256 us (25%)
  Pallas kernels  111 us (11%)
  local copies, waits for them, and re-layouts  38.6 us (4%)
  other arithmetic  28.8 us (3%)
  starting transfers between devices  28 us (3%)
    all_to_all x2, waiting for transfers between devices, local_layer(): lax.all_to_all(send.reshape((group_size, part) + tail), 'ep', 0, 0, tiled...  288 us
    all_to_all x2, waiting for transfers between devices, local_layer(): back.append((idx, lax.all_to_all(contrib, 'ep', 0, 0, tiled=True)))  263 us
    dot_general x2, matrix products, local_layer(): jnp.dot(got.reshape(rows, model_width), up_loc[0], preferred_element_type...  146 us
    dot_general x2, matrix products, local_layer(): out = jnp.dot(hidden, down_loc[0], preferred_element_type=jnp.float32)  110 us
    pallas_call x2, Pallas kernels, combine_rows(): pl.pallas_call(combine_kernel, grid_spec=pltpu.PrefetchScalarGridSpec(num...  69.1 us
    pallas_call x2, Pallas kernels, pack_rows(): pl.pallas_call(pack_kernel, grid_spec=pltpu.PrefetchScalarGridSpec(num_sc...  42.2 us
    unnamed x21, local copies, waits for them, and re-layouts  37.8 us
  transfers between devices with their start and end apart: 5, of which 4 were waited for; matrix products, arithmetic and copies ran while one was open for 29% of the time, Pallas kernels for 6%

profile of v2, /device:TPU:107, one launch (start us, length us, event | category | flops | bytes accessed | tf_op | source)
XLA Modules:
  0.0 1013.5 jit_solution(5773117085885931157)
XLA Ops:
  0.0 0.8 multiply_add_fusion.1
  1.4 0.8 concatenate.7
  2.2 6.4 sort.15
  8.6 0.7 broadcast_subtract_fusion
  9.3 7.7 all-to-all-start
  17.0 8.9 copy.9
  26.0 0.6 copy-done.2
  26.6 0.6 broadcast_minimum_fusion.1.idx_ref
  27.2 21.1 %shard_map.55 = bf16[8192,8,128]{2,1,0:T(8,128)(2,1)} custom-call(s32[8192]{0:T(1024)} %broadcast_minimum_fusion.1.idx_ref, bf16[4096,8,128]{2,1,0:T(8,128)(2,1)} %bitcast.79), custom_call_target="tpu_custom_call" | custom-call | flops 33554432 | bytes 33554432 | tf_op jit(solution)/shard_map/pallas_call | solution.py:32
  48.3 6.3 all-to-all-start.1
  54.7 0.6 copy.14
  55.4 0.6 copy-done.3
  56.0 0.6 broadcast_minimum_fusion.idx_ref
  56.6 21.1 %shard_map.57 = bf16[8192,8,128]{2,1,0:T(8,128)(2,1)} custom-call(s32[8192]{0:T(1024)} %broadcast_minimum_fusion.idx_ref, bf16[4096,8,128]{2,1,0:T(8,128)(2,1)} %bitcast.80), custom_call_target="tpu_custom_call" | custom-call | flops 33554432 | bytes 33554432 | tf_op jit(solution)/shard_map/pallas_call | solution.py:32
  77.7 200.2 %all-to-all-done.1 = bf16[32,256,8,128]{3,2,1,0:T(8,128)(2,1)} async-done(((bf16[32,256,8,128]{3,2,1,0:T(8,128)(2,1)}), bf16[32,256,8,128]{3,2,1,0:T(8,128)(2,1)}, u32[]{:S(2)}, u32[]{:S(2)}) %all-to-all-start.1) | async-done | bytes 16777248 | tf_op jit(solution)/shard_map/all_to_all | solution.py:125
  277.9 5.7 all-to-all-start.3
  283.6 72.8 %fusion.7.clone.6 = bf16[8192,2816]{1,0:T(8,128)(2,1)} fusion(bf16[1024,8,8,128]{3,2,1,0:T(8,128)(2,1)} %bitcast.15, bf16[1,1024,2816]{2,1,0:T(8,128)(2,1)} %param.8), kind=kOutput, calls=%fused_computation.9.clone.clone.clone.clone.clone.1 | convolution fusion | flops 47452258304 | bytes 68681728 | tf_op jit(solution)/shard_map/dot_general | solution.py:129
  356.4 54.9 %fusion.24 = bf16[1024,8,8,128]{3,1,2,0:T(8,128)(2,1)S(1)} fusion(f32[8192]{0:T(1024)S(1)} %bitcast.96, bf16[1,2816,1024]{2,1,0:T(8,128)(2,1)} %param.9, bf16[8192,2816]{1,0:T(8,128)(2,1)} %fusion.7.clone.6), kind=kOutput, calls=%fused_computation.25 | convolution fusion | flops 47261417472 | bytes 68714496 | tf_op jit(solution)/shard_map/dot_general | solution.py:130
  411.4 9.0 copy.12
  420.4 87.3 %all-to-all-done.3 = bf16[32,256,8,128]{3,2,1,0:T(8,128)(2,1)} async-done(((bf16[32,256,8,128]{3,2,1,0:T(8,128)(2,1)}), bf16[32,256,8,128]{3,2,1,0:T(8,128)(2,1)}, u32[]{:S(2)}, u32[]{:S(2)}) %all-to-all-start.3) | async-done | bytes 16777248 | tf_op jit(solution)/shard_map/all_to_all | solution.py:125
  507.7 4.3 all-to-all-start.2
  512.0 72.8 %fusion.15.clone.4 = bf16[8192,2816]{1,0:T(8,128)(2,1)} fusion(bf16[1024,8,8,128]{3,2,1,0:T(8,128)(2,1)} %bitcast.23, bf16[1,1024,2816]{2,1,0:T(8,128)(2,1)} %param.8), kind=kOutput, calls=%fused_computation.17.clone.clone.clone.clone.clone | convolution fusion | flops 47452258304 | bytes 68681728 | tf_op jit(solution)/shard_map/dot_general | solution.py:129
  584.8 55.0 %fusion.27 = bf16[1024,8,8,128]{3,1,2,0:T(8,128)(2,1)S(1)} fusion(f32[8192]{0:T(1024)S(1)} %bitcast.95, bf16[1,2816,1024]{2,1,0:T(8,128)(2,1)} %param.9, bf16[8192,2816]{1,0:T(8,128)(2,1)} %fusion.15.clone.4), kind=kOutput, calls=%fused_computation.26 | convolution fusion | flops 47261417472 | bytes 68714496 | tf_op jit(solution)/shard_map/dot_general | solution.py:130
  639.8 9.0 copy.15
  648.8 87.1 %all-to-all-done.2.ret_ref = bf16[32,256,8,128]{3,2,1,0:T(8,128)(2,1)} async-done(((bf16[32,256,8,128]{3,2,1,0:T(8,128)(2,1)}), bf16[32,256,8,128]{3,2,1,0:T(8,128)(2,1)}, u32[]{:S(2)}, u32[]{:S(2)}) %all-to-all-start.2) | async-done | bytes 16777248 | tf_op jit(solution)/shard_map/all_to_all | solution.py:133
  735.9 4.1 all-to-all-start.4
  740.0 9.5 bitcast_convert_fusion.base_ref
  750.1 36.4 %shard_map.56.base_ref = f32[4096,8,128]{2,1,0:T(8,128)} custom-call(s32[8192]{0:T(1024)} %bitcast.88, s32[32]{0:T(128)} %get-tuple-element.15.cnt_ref, f32[4096,8,128]{2,1,0:T(8,128)} %bitcast_convert_fusion.base_ref, bf16[32,256,8,128]{3,2,1,0:T(8,128)(2,1)} %all-to-all-done.2.ret_ref), custom_call_target="tpu_custom_call" | custom-call | flops 33554432 | bytes 50331648 | tf_op jit(solution)/shard_map/pallas_call | solution.py:76
  786.5 176.0 %all-to-all-done.4.ret_ref = bf16[32,256,8,128]{3,2,1,0:T(8,128)(2,1)} async-done(((bf16[32,256,8,128]{3,2,1,0:T(8,128)(2,1)}), bf16[32,256,8,128]{3,2,1,0:T(8,128)(2,1)}, u32[]{:S(2)}, u32[]{:S(2)}) %all-to-all-start.4) | async-done | bytes 16777248 | tf_op jit(solution)/shard_map/all_to_all | solution.py:133
  962.5 32.7 %shard_map.58 = f32[4096,8,128]{2,1,0:T(8,128)} custom-call(s32[8192]{0:T(1024)} %bitcast.90, s32[32]{0:T(128)} %get-tuple-element.16.cnt_ref, f32[4096,8,128]{2,1,0:T(8,128)} %shard_map.56.base_ref, bf16[32,256,8,128]{3,2,1,0:T(8,128)(2,1)} %all-to-all-done.4.ret_ref), custom_call_target="tpu_custom_call" | custom-call | flops 33554432 | bytes 50331648 | tf_op jit(solution)/shard_map/pallas_call | solution.py:76
  995.3 8.9 convert_element_type.38
  1004.2 8.9 copy.41
  (25 shorter events, 1.3 us)
Async XLA Ops:
  9.3 16.6 %all-to-all-start = ((s32[32,1,512]{2,1,0:T(1,128)}), s32[32,1,512]{2,1,0:T(1,128)S(1)}, u32[]{:S(2)}, u32[]{:S(2)}) async-start(s32[32,1,512]{2,1,0:T(1,128)} %broadcast_subtract_fusion), calls=%async_computation | async-start | bytes 131072 | tf_op jit(solution)/shard_map/all_to_all | solution.py:116
  26.0 51.7 %copy-start = (s32[32,1,512]{2,1,0:T(1,128)}, s32[32,1,512]{2,1,0:T(1,128)S(1)}, u32[]{:S(2)}) copy-start(s32[32,1,512]{2,1,0:T(1,128)S(1)} %all-to-all-done) | copy-start | bytes 196612
  26.0 0.6 copy-start.2
  48.3 229.6 %all-to-all-start.1 = ((bf16[32,256,8,128]{3,2,1,0:T(8,128)(2,1)}), bf16[32,256,8,128]{3,2,1,0:T(8,128)(2,1)}, u32[]{:S(2)}, u32[]{:S(2)}) async-start(bf16[32,256,8,128]{3,2,1,0:T(8,128)(2,1)} %bitcast.81), calls=%async_computation.1 | async-start | bytes 33554432 | tf_op jit(solution)/shard_map/all_to_all | solution.py:125
  55.4 0.6 copy-start.3
  277.9 229.8 %all-to-all-start.3 = ((bf16[32,256,8,128]{3,2,1,0:T(8,128)(2,1)}), bf16[32,256,8,128]{3,2,1,0:T(8,128)(2,1)}, u32[]{:S(2)}, u32[]{:S(2)}) async-start(bf16[32,256,8,128]{3,2,1,0:T(8,128)(2,1)} %bitcast.83), calls=%async_computation.3 | async-start | bytes 33554432 | tf_op jit(solution)/shard_map/all_to_all | solution.py:125
  507.7 228.2 %all-to-all-start.2 = ((bf16[32,256,8,128]{3,2,1,0:T(8,128)(2,1)}), bf16[32,256,8,128]{3,2,1,0:T(8,128)(2,1)}, u32[]{:S(2)}, u32[]{:S(2)}) async-start(bf16[32,256,8,128]{3,2,1,0:T(8,128)(2,1)} %bitcast.84), calls=%async_computation.2 | async-start | bytes 33554432 | tf_op jit(solution)/shard_map/all_to_all | solution.py:133
  512.0 72.8 %copy-start.4 = (f32[4,2,8,128]{3,1,2,0:T(2,128)S(1)}, f32[4,2,8,128]{3,1,2,0:T(2,128)}, u32[]{:S(2)}) copy-start(f32[4,2,8,128]{3,1,2,0:T(2,128)} %copy.14) | copy-start | bytes 98308
  648.8 100.7 %copy-start.1 = (s32[32,1,512]{2,1,0:T(1,128)S(1)}, s32[32,1,512]{2,1,0:T(1,128)}, u32[]{:S(2)}) copy-start(s32[32,1,512]{2,1,0:T(1,128)} %copy-done) | copy-start | bytes 196612
  735.9 226.6 %all-to-all-start.4 = ((bf16[32,256,8,128]{3,2,1,0:T(8,128)(2,1)}), bf16[32,256,8,128]{3,2,1,0:T(8,128)(2,1)}, u32[]{:S(2)}, u32[]{:S(2)}) async-start(bf16[32,256,8,128]{3,2,1,0:T(8,128)(2,1)} %bitcast.82), calls=%async_computation.4 | async-start | bytes 33554432 | tf_op jit(solution)/shard_map/all_to_all | solution.py:133

commit v3 on v1

v3 whole, which is shorter than its diff:
```python
import functools
import math

import jax
import jax.numpy as jnp
from jax import lax
from jax.experimental import pallas as pl
from jax.experimental.pallas import tpu as pltpu
from jax.sharding import PartitionSpec as P

LANES = 128
BATCH = 8
VMEM_LIMIT = 60 * 1024 * 1024
SEND_SLOTS = 8
OUT_SLOTS = 6
AHEAD = 6
STRIDE = 13
COLS = 256
STEP = 128


def peers(k, group, side):
    me = lax.axis_index("ep")
    d = (k * STRIDE) % group
    dy, dx, dc = d // (2 * side), (d // 2) % side, d % 2
    y, x, c = me // (2 * side), (me // 2) % side, me % 2
    to = (((y + dy) % side) * side + (x + dx) % side) * 2 + (c + dc) % 2
    frm = (((y + side - dy) % side) * side + (x + side - dx) % side) * 2 + (c + 2 - dc) % 2
    return to, frm


def moe_kernel(group, side, idx_ref, x_ref, up_ref, down_ref, gate_ref, recv_ref, ret_ref,
               rows, send, blk, gblk, hid, out, send_sem, out_sem, recv_sem, ret_sem, load_sem):
    me = lax.axis_index("ep")
    cap, sub = rows.shape[0], rows.shape[1]

    barrier = pltpu.get_barrier_semaphore()

    def hello(d, _):
        pl.semaphore_signal(barrier, inc=1, device_id={"ep": (me + d) % group}, device_id_type=pl.DeviceIdType.MESH)
        return 0

    lax.fori_loop(1, group, hello, 0)
    pl.semaphore_wait(barrier, group - 1)

    def dispatch(k):
        to, _ = peers(k, group, side)
        return pltpu.make_async_remote_copy(
            src_ref=send.at[k % SEND_SLOTS], dst_ref=recv_ref.at[me], send_sem=send_sem.at[k % SEND_SLOTS],
            recv_sem=recv_sem.at[k], device_id={"ep": to}, device_id_type=pl.DeviceIdType.MESH)

    def give_back(k):
        _, frm = peers(k, group, side)
        return pltpu.make_async_remote_copy(
            src_ref=out.at[k % OUT_SLOTS], dst_ref=ret_ref.at[me], send_sem=out_sem.at[k % OUT_SLOTS],
            recv_sem=ret_sem.at[k], device_id={"ep": frm}, device_id_type=pl.DeviceIdType.MESH)

    def pack(to, dst):
        def pick(b, _):
            vals = [x_ref[idx_ref[to, b * BATCH + j]].astype(jnp.float32) for j in range(BATCH)]
            for j in range(BATCH):
                rows[b * BATCH + j] = vals[j]
            return 0

        lax.fori_loop(0, cap // BATCH, pick, 0)

        def flat(b, _):
            at = pl.ds(b * STEP, STEP)
            for s in range(sub):
                dst[at, s * LANES:(s + 1) * LANES] = rows[at, s, :].astype(jnp.bfloat16)
            return 0

        lax.fori_loop(0, cap // STEP, flat, 0)

    def pack_and_send(k):
        to, _ = peers(k, group, side)

        @pl.when(k > SEND_SLOTS)
        def _():
            dispatch(k - SEND_SLOTS).wait_send()

        pack(to, send.at[k % SEND_SLOTS])
        dispatch(k).start()

    def ffn_up():
        def up(f, _):
            at = pl.ds(pl.multiple_of(f * COLS, COLS), COLS)
            z = jnp.dot(blk[...], up_ref[:, at], preferred_element_type=jnp.float32)
            hid[:, at] = jax.nn.gelu(z, approximate=True).astype(jnp.bfloat16)
            return 0

        lax.fori_loop(0, up_ref.shape[1] // COLS, up, 0)

    def ffn_down(slot):
        for n in range(down_ref.shape[1] // COLS):
            o = jnp.dot(hid[...], down_ref[:, n * COLS:(n + 1) * COLS], preferred_element_type=jnp.float32)
            for t in range(COLS // LANES):
                rows[:, n * (COLS // LANES) + t, :] = o[:, t * LANES:(t + 1) * LANES] * gblk[...]

        def tile(b, _):
            at = pl.ds(b * STEP, STEP)
            out[slot, at] = rows[at].astype(jnp.bfloat16)
            return 0

        lax.fori_loop(0, cap // STEP, tile, 0)

    def own():
        load_gate = pltpu.make_async_copy(gate_ref.at[me], gblk, load_sem.at[1])
        load_gate.start()
        pack(me, blk)
        load_gate.wait()
        ffn_up()
        ffn_down(0)
        keep = pltpu.make_async_copy(out.at[0], ret_ref.at[me], load_sem.at[0])
        keep.start()
        keep.wait()

    def expert(k):
        to, frm = peers(k, group, side)
        pltpu.make_async_remote_copy(
            src_ref=send.at[0], dst_ref=recv_ref.at[frm], send_sem=send_sem.at[0], recv_sem=recv_sem.at[k],
            device_id={"ep": to}, device_id_type=pl.DeviceIdType.MESH).wait_recv()
        load_rows = pltpu.make_async_copy(recv_ref.at[frm], blk, load_sem.at[0])
        load_gate = pltpu.make_async_copy(gate_ref.at[frm], gblk, load_sem.at[1])
        load_rows.start()
        load_gate.start()
        load_rows.wait()
        load_gate.wait()
        ffn_up()

        @pl.when(k > OUT_SLOTS)
        def _():
            give_back(k - OUT_SLOTS).wait_send()

        ffn_down(k % OUT_SLOTS)
        give_back(k).start()

    def first(k, _):
        pack_and_send(k)
        return 0

    def step(k, _):
        @pl.when(k + AHEAD < group)
        def _():
            pack_and_send(k + AHEAD)

        expert(k)
        return 0

    lax.fori_loop(1, min(AHEAD + 1, group), first, 0)
    own()
    lax.fori_loop(1, group, step, 0)

    def drain_send(k, _):
        dispatch(k).wait_send()
        return 0

    def drain_out(k, _):
        give_back(k).wait_send()
        return 0

    def drain_ret(k, _):
        to, _ = peers(k, group, side)
        pltpu.make_async_remote_copy(
            src_ref=out.at[0], dst_ref=ret_ref.at[to], send_sem=out_sem.at[0], recv_sem=ret_sem.at[k],
            device_id={"ep": to}, device_id_type=pl.DeviceIdType.MESH).wait_recv()
        return 0

    lax.fori_loop(max(group - SEND_SLOTS, 1), group, drain_send, 0)
    lax.fori_loop(max(group - OUT_SLOTS, 1), group, drain_out, 0)
    lax.fori_loop(1, group, drain_ret, 0)


def moe_exchange(group, idx, x3, up, down, gates):
    side = math.isqrt(group // 2)
    assert 2 * side * side == group
    cap = idx.shape[1]
    tail = x3.shape[1:]
    width, hidden = up.shape
    any_spec = pl.BlockSpec(memory_space=pl.ANY)
    vmem_spec = pl.BlockSpec(memory_space=pltpu.VMEM)
    _, ret = pl.pallas_call(
        functools.partial(moe_kernel, group, side),
        in_specs=[pl.BlockSpec(memory_space=pltpu.SMEM), vmem_spec, vmem_spec, vmem_spec, any_spec],
        out_specs=[any_spec, any_spec],
        out_shape=[jax.ShapeDtypeStruct((group, cap, width), x3.dtype), jax.ShapeDtypeStruct((group, cap) + tail, x3.dtype)],
        scratch_shapes=[
            pltpu.VMEM((cap,) + tail, jnp.float32),
            pltpu.VMEM((SEND_SLOTS, cap, width), x3.dtype),
            pltpu.VMEM((cap, width), x3.dtype),
            pltpu.VMEM((cap, LANES), jnp.float32),
            pltpu.VMEM((cap, hidden), x3.dtype),
            pltpu.VMEM((OUT_SLOTS, cap) + tail, x3.dtype),
            pltpu.SemaphoreType.DMA((SEND_SLOTS,)),
            pltpu.SemaphoreType.DMA((OUT_SLOTS,)),
            pltpu.SemaphoreType.DMA((group,)),
            pltpu.SemaphoreType.DMA((group,)),
            pltpu.SemaphoreType.DMA((2,)),
        ],
        compiler_params=pltpu.CompilerParams(collective_id=0, has_side_effects=True, vmem_limit_bytes=VMEM_LIMIT),
        cost_estimate=pl.CostEstimate(flops=4 * group * cap * width * hidden, bytes_accessed=4 * group * cap * width, transcendentals=0),
    )(idx, x3, up, down, gates)
    return ret


def combine_kernel(idx_ref, cnt_ref, x_ref, ret_ref, out_ref, acc):
    g = pl.program_id(0)
    part = ret_ref.shape[0]
    tok, width = x_ref.shape
    sub = width // LANES

    @pl.when(g == 0)
    def _():
        def load(b, _):
            at = pl.ds(b * STEP, STEP)
            for s in range(sub):
                acc[at, s, :] = x_ref[at, s * LANES:(s + 1) * LANES].astype(jnp.float32)
            return 0

        lax.fori_loop(0, tok // STEP, load, 0)

    def body(b, _):
        at = [idx_ref[g * part + b * BATCH + j] for j in range(BATCH)]
        sums = [acc[at[j]] + ret_ref[b * BATCH + j].astype(jnp.float32) for j in range(BATCH)]
        for j in range(BATCH):
            acc[at[j]] = sums[j]
        return 0

    lax.fori_loop(0, (cnt_ref[g] + BATCH - 1) // BATCH, body, 0)

    @pl.when(g == pl.num_programs(0) - 1)
    def _():
        def store(b, _):
            at = pl.ds(b * STEP, STEP)
            for s in range(sub):
                out_ref[at, s * LANES:(s + 1) * LANES] = acc[at, s, :].astype(jnp.bfloat16)
            return 0

        lax.fori_loop(0, tok // STEP, store, 0)


def combine_rows(x_loc, ret, idx, cnt):
    group, part = ret.shape[:2]
    tail = ret.shape[2:]
    tok = x_loc.shape[0]
    whole = pl.BlockSpec(x_loc.shape, lambda g, idx, cnt: (0, 0))
    return pl.pallas_call(
        combine_kernel,
        grid_spec=pltpu.PrefetchScalarGridSpec(
            num_scalar_prefetch=2,
            grid=(group,),
            in_specs=[whole, pl.BlockSpec((None, part) + tail, lambda g, idx, cnt: (g, 0, 0, 0))],
            out_specs=whole,
            scratch_shapes=[pltpu.VMEM((tok + 8,) + tail, jnp.float32)],
        ),
        out_shape=jax.ShapeDtypeStruct(x_loc.shape, x_loc.dtype),
        compiler_params=pltpu.CompilerParams(vmem_limit_bytes=VMEM_LIMIT),
        cost_estimate=pl.CostEstimate(flops=group * part * 4096, bytes_accessed=group * part * 4096, transcendentals=0),
    )(idx, cnt, x_loc, ret)


def solution(mesh):
    group_size = mesh.shape["ep"]

    def local_layer(x_loc, sel_loc, gate_loc, up_loc, down_loc):
        tok_loc, model_width = x_loc.shape
        tail = (model_width // LANES, LANES)
        entry_count = sel_loc.shape[0] * sel_loc.shape[1]
        pair_cap = 2 * entry_count // group_size
        sel = sel_loc.reshape(entry_count)
        dev_ids = jnp.arange(group_size, dtype=jnp.int32)
        src_dev = sel // tok_loc
        counts = jnp.sum((src_dev[:, None] == dev_ids[None, :]).astype(jnp.int32), axis=0)
        lower = dev_ids[:, None] >= dev_ids[None, :]
        free_end = jnp.sum(jnp.where(lower, (pair_cap - counts)[None, :], 0), axis=1)
        fill_ids = jnp.arange(group_size * pair_cap - entry_count, dtype=jnp.int32)
        fill_dev = jnp.sum((free_end[None, :] <= fill_ids[:, None]).astype(jnp.int32), axis=1)
        keys = jnp.concatenate([sel + src_dev * tok_loc, fill_dev * (2 * tok_loc) + tok_loc])
        gates = jnp.concatenate([gate_loc.reshape(entry_count), jnp.zeros(fill_ids.shape, jnp.float32)])
        keys, gates = lax.sort((keys, gates), num_keys=1, is_stable=False)
        request = keys.reshape(group_size, pair_cap) - dev_ids[:, None] * (2 * tok_loc)
        gates = jnp.broadcast_to(gates.reshape(group_size, pair_cap)[:, :, None], (group_size, pair_cap, LANES))
        wanted = lax.all_to_all(request, "ep", 0, 0, tiled=True)
        filled = jnp.sum((wanted < tok_loc).astype(jnp.int32), axis=1)
        x3 = x_loc.reshape((tok_loc,) + tail)
        ret = moe_exchange(group_size, jnp.minimum(wanted, tok_loc - 1), x3, up_loc[0], down_loc[0], gates)
        return combine_rows(x_loc, ret, wanted.reshape(group_size * pair_cap), filled)

    row_spec = P(("dp", "ep"), None)
    weight_spec = P("ep", None, None)
    return jax.shard_map(local_layer, mesh=mesh, in_specs=(row_spec, row_spec, row_spec, weight_spec, weight_spec), out_specs=row_spec, check_vma=False)
```

time: 1090 us -> 1120 us (1.028)
  the two profiles are of different devices: /device:TPU:107 before, /device:TPU:116 now
where the time goes in v3:
time: 1120 us
  Pallas kernels  1090 us (97%)
  local copies, waits for them, and re-layouts  14.2 us (1%)
  other arithmetic  11.3 us (1%)
    pallas_call x1, Pallas kernels, moe_exchange(): pl.pallas_call(functools.partial(moe_kernel, group, side), in_specs=[pl.B...  1020 us
    pallas_call x1, Pallas kernels, combine_rows(): pl.pallas_call(combine_kernel, grid_spec=pltpu.PrefetchScalarGridSpec(num...  63.4 us
  transfers between devices with their start and end apart: 1, of which 0 were waited for; matrix products, arithmetic and copies ran while one was open for 1% of the time, Pallas kernels for 0%

profile of v3, /device:TPU:116, one launch (start us, length us, event | category | flops | bytes accessed | tf_op | source)
XLA Modules:
  0.0 1118.3 jit_solution(9838133888247062917)
XLA Ops:
  0.0 0.8 multiply_add_fusion.1
  0.8 0.2 convert_reduce_fusion.1
  1.0 0.1 select_reduce_fusion
  1.1 0.2 convert_reduce_fusion
  1.4 0.8 concatenate.7
  2.2 6.4 sort.15
  8.6 0.7 broadcast_subtract_fusion
  9.3 6.7 all-to-all-start
  16.1 8.9 copy.8
  25.0 0.0 all-to-all-done
  25.0 0.0 copy-start
  25.0 0.7 fusion.1.idx_ref
  25.7 4.5 broadcast_in_dim.19.gate_ref
  30.2 1022.7 %shard_map.55 = (bf16[32,512,1024]{2,1,0:T(8,128)(2,1)}, bf16[32,512,8,128]{3,2,1,0:T(8,128)(2,1)}) custom-call(s32[32,512]{1,0:T(8,128)} %fusion.1.idx_ref, bf16[4096,8,128]{2,1,0:T(8,128)(2,1)} %bitcast.11, bf16[1024,2816]{1,0:T(8,128)(2,1)} %bitcast.16, bf16[2816,1024]{1,0:T(8,128)(2,1)} %bitcast.17, f32[32,512,128]{2,1,0:T(8,128)} %broadcast_in_dim.19.gate_ref), custom_call_target="tpu_custom_call" | custom-call | flops 188978561024 | bytes 67108864 | tf_op jit(solution)/shard_map/pallas_call | solution.py:182
  1052.9 0.0 copy-done
  1052.9 2.1 fusion.cnt_ref
  1055.0 63.4 %shard_map.56 = bf16[4096,1024]{1,0:T(8,128)(2,1)} custom-call(s32[16384]{0:T(1024)} %bitcast.12, s32[32]{0:T(128)} %fusion.cnt_ref, bf16[4096,1024]{1,0:T(8,128)(2,1)} %x_ref.1, bf16[32,512,8,128]{3,2,1,0:T(8,128)(2,1)} %get-tuple-element.10.ret_ref), custom_call_target="tpu_custom_call" | custom-call | flops 67108864 | bytes 67108864 | tf_op jit(solution)/shard_map/pallas_call | solution.py:247
  (5 shorter events, 0.0 us)
Async XLA Ops:
  9.3 15.7 %all-to-all-start = ((s32[32,1,512]{2,1,0:T(1,128)}), s32[32,1,512]{2,1,0:T(1,128)S(1)}, u32[]{:S(2)}, u32[]{:S(2)}) async-start(s32[32,1,512]{2,1,0:T(1,128)} %broadcast_subtract_fusion), calls=%async_computation | async-start | bytes 131072 | tf_op jit(solution)/shard_map/all_to_all | solution.py:283
  25.0 1027.8 %copy-start = (s32[32,1,512]{2,1,0:T(1,128)}, s32[32,1,512]{2,1,0:T(1,128)S(1)}, u32[]{:S(2)}) copy-start(s32[32,1,512]{2,1,0:T(1,128)S(1)} %all-to-all-done) | copy-start | bytes 196612

commit v4 on v3

--- a/solution.py
+++ b/solution.py
@@ -10,10 +10,11 @@
 
 LANES = 128
 BATCH = 8
+ADD_BATCH = 16
 VMEM_LIMIT = 60 * 1024 * 1024
-SEND_SLOTS = 8
-OUT_SLOTS = 6
-AHEAD = 6
+SEND_SLOTS = 14
+OUT_SLOTS = 10
+AHEAD = 13
 STRIDE = 13
 COLS = 256
 STEP = 128
@@ -220,13 +221,13 @@
         lax.fori_loop(0, tok // STEP, load, 0)
 
     def body(b, _):
-        at = [idx_ref[g * part + b * BATCH + j] for j in range(BATCH)]
-        sums = [acc[at[j]] + ret_ref[b * BATCH + j].astype(jnp.float32) for j in range(BATCH)]
-        for j in range(BATCH):
+        at = [idx_ref[g * part + b * ADD_BATCH + j] for j in range(ADD_BATCH)]
+        sums = [acc[at[j]] + ret_ref[b * ADD_BATCH + j].astype(jnp.float32) for j in range(ADD_BATCH)]
+        for j in range(ADD_BATCH):
             acc[at[j]] = sums[j]
         return 0
 
-    lax.fori_loop(0, (cnt_ref[g] + BATCH - 1) // BATCH, body, 0)
+    lax.fori_loop(0, (cnt_ref[g] + ADD_BATCH - 1) // ADD_BATCH, body, 0)
 
     @pl.when(g == pl.num_programs(0) - 1)
     def _():

time: 1120 us -> 1030 us (0.920)
  the two profiles are of different devices: /device:TPU:116 before, /device:TPU:103 now
where the time goes in v4:
time: 1030 us
  Pallas kernels  994 us (97%)
  local copies, waits for them, and re-layouts  14.2 us (1%)
  other arithmetic  11.3 us (1%)
    pallas_call x1, Pallas kernels, moe_exchange(): pl.pallas_call(functools.partial(moe_kernel, group, side), in_specs=[pl.B...  928 us
    pallas_call x1, Pallas kernels, combine_rows(): pl.pallas_call(combine_kernel, grid_spec=pltpu.PrefetchScalarGridSpec(num...  66 us
  transfers between devices with their start and end apart: 1, of which 0 were waited for; matrix products, arithmetic and copies ran while one was open for 1% of the time, Pallas kernels for 0%

profile of v4, /device:TPU:103, one launch (start us, length us, event | category | flops | bytes accessed | tf_op | source)
XLA Modules:
  0.0 1027.6 jit_solution(5998562368072976768)
XLA Ops:
  0.0 0.8 multiply_add_fusion.1
  0.8 0.2 convert_reduce_fusion.1
  1.0 0.1 select_reduce_fusion
  1.1 0.2 convert_reduce_fusion
  1.4 0.8 concatenate.7
  2.2 6.4 sort.15
  8.6 0.7 broadcast_subtract_fusion
  9.3 8.0 all-to-all-start
  17.4 8.9 copy.8
  26.3 0.0 all-to-all-done
  26.3 0.0 copy-start
  26.3 0.7 fusion.1.idx_ref
  27.0 4.5 broadcast_in_dim.19.gate_ref
  31.5 928.0 %shard_map.55 = (bf16[32,512,1024]{2,1,0:T(8,128)(2,1)}, bf16[32,512,8,128]{3,2,1,0:T(8,128)(2,1)}) custom-call(s32[32,512]{1,0:T(8,128)} %fusion.1.idx_ref, bf16[4096,8,128]{2,1,0:T(8,128)(2,1)} %bitcast.11, bf16[1024,2816]{1,0:T(8,128)(2,1)} %bitcast.16, bf16[2816,1024]{1,0:T(8,128)(2,1)} %bitcast.17, f32[32,512,128]{2,1,0:T(8,128)} %broadcast_in_dim.19.gate_ref), custom_call_target="tpu_custom_call" | custom-call | flops 188978561024 | bytes 67108864 | tf_op jit(solution)/shard_map/pallas_call | solution.py:183
  959.5 0.0 copy-done
  959.5 2.1 fusion.cnt_ref
  961.6 66.0 %shard_map.56 = bf16[4096,1024]{1,0:T(8,128)(2,1)} custom-call(s32[16384]{0:T(1024)} %bitcast.12, s32[32]{0:T(128)} %fusion.cnt_ref, bf16[4096,1024]{1,0:T(8,128)(2,1)} %x_ref.1, bf16[32,512,8,128]{3,2,1,0:T(8,128)(2,1)} %get-tuple-element.10.ret_ref), custom_call_target="tpu_custom_call" | custom-call | flops 67108864 | bytes 67108864 | tf_op jit(solution)/shard_map/pallas_call | solution.py:248
  (5 shorter events, 0.0 us)
Async XLA Ops:
  9.3 17.0 %all-to-all-start = ((s32[32,1,512]{2,1,0:T(1,128)}), s32[32,1,512]{2,1,0:T(1,128)S(1)}, u32[]{:S(2)}, u32[]{:S(2)}) async-start(s32[32,1,512]{2,1,0:T(1,128)} %broadcast_subtract_fusion), calls=%async_computation | async-start | bytes 131072 | tf_op jit(solution)/shard_map/all_to_all | solution.py:284
  26.3 933.1 %copy-start = (s32[32,1,512]{2,1,0:T(1,128)}, s32[32,1,512]{2,1,0:T(1,128)S(1)}, u32[]{:S(2)}) copy-start(s32[32,1,512]{2,1,0:T(1,128)S(1)} %all-to-all-done) | copy-start | bytes 196612

commit v5 on v2

--- a/solution.py
+++ b/solution.py
@@ -10,6 +10,8 @@
 CHUNKS = 2
 LANES = 128
 BATCH = 8
+ADD_BATCH = 16
+STEP = 128
 VMEM_LIMIT = 60 * 1024 * 1024
 
 
@@ -43,7 +45,7 @@
     )(idx, x3)
 
 
-def combine_kernel(idx_ref, cnt_ref, base_ref, ret_ref, out_ref, acc, sem):
+def combine_kernel(last, idx_ref, cnt_ref, base_ref, ret_ref, out_ref, acc, sem):
     g = pl.program_id(0)
     part = ret_ref.shape[0]
     tok = base_ref.shape[0]
@@ -55,26 +57,36 @@
         load.wait()
 
     def body(b, _):
-        at = [idx_ref[g * part + b * BATCH + j] for j in range(BATCH)]
-        sums = [acc[at[j]] + ret_ref[b * BATCH + j].astype(jnp.float32) for j in range(BATCH)]
-        for j in range(BATCH):
+        at = [idx_ref[g * part + b * ADD_BATCH + j] for j in range(ADD_BATCH)]
+        sums = [acc[at[j]] + ret_ref[b * ADD_BATCH + j].astype(jnp.float32) for j in range(ADD_BATCH)]
+        for j in range(ADD_BATCH):
             acc[at[j]] = sums[j]
         return 0
 
-    lax.fori_loop(0, (cnt_ref[g] + BATCH - 1) // BATCH, body, 0)
+    lax.fori_loop(0, (cnt_ref[g] + ADD_BATCH - 1) // ADD_BATCH, body, 0)
 
     @pl.when(g == pl.num_programs(0) - 1)
     def _():
-        store = pltpu.make_async_copy(acc.at[pl.ds(0, tok)], out_ref, sem)
-        store.start()
-        store.wait()
+        if last:
+            def flat(b, _):
+                at = pl.ds(b * STEP, STEP)
+                for s in range(acc.shape[1]):
+                    out_ref[at, s * LANES:(s + 1) * LANES] = acc[at, s, :].astype(jnp.bfloat16)
+                return 0
+
+            lax.fori_loop(0, tok // STEP, flat, 0)
+        else:
+            store = pltpu.make_async_copy(acc.at[pl.ds(0, tok)], out_ref, sem)
+            store.start()
+            store.wait()
 
 
-def combine_rows(base, ret, idx, cnt):
+def combine_rows(base, ret, idx, cnt, last):
     group, part = ret.shape[:2]
     tail = base.shape[1:]
+    flat = (base.shape[0], tail[0] * tail[1])
     return pl.pallas_call(
-        combine_kernel,
+        functools.partial(combine_kernel, last),
         grid_spec=pltpu.PrefetchScalarGridSpec(
             num_scalar_prefetch=2,
             grid=(group,),
@@ -82,10 +94,10 @@
                 pl.BlockSpec(memory_space=pl.ANY),
                 pl.BlockSpec((None, part) + tail, lambda g, idx, cnt: (g, 0, 0, 0)),
             ],
-            out_specs=pl.BlockSpec(memory_space=pl.ANY),
+            out_specs=pl.BlockSpec(flat, lambda g, idx, cnt: (0, 0)) if last else pl.BlockSpec(memory_space=pl.ANY),
             scratch_shapes=[pltpu.VMEM((base.shape[0] + 8,) + tail, jnp.float32), pltpu.SemaphoreType.DMA],
         ),
-        out_shape=jax.ShapeDtypeStruct(base.shape, jnp.float32),
+        out_shape=jax.ShapeDtypeStruct(flat, jnp.bfloat16) if last else jax.ShapeDtypeStruct(base.shape, jnp.float32),
         compiler_params=pltpu.CompilerParams(vmem_limit_bytes=VMEM_LIMIT),
         cost_estimate=pl.CostEstimate(flops=group * part * 4096, bytes_accessed=group * part * 6144, transcendentals=0),
     )(idx, cnt, base, ret)
@@ -133,8 +145,8 @@
             back.append((idx, lax.all_to_all(contrib, "ep", 0, 0, tiled=True)))
         acc = x3.astype(jnp.float32)
         for k, (idx, ret) in enumerate(back):
-            acc = combine_rows(acc, ret, idx, jnp.clip(filled - k * part, 0, part))
-        return acc.reshape(tok_loc, model_width).astype(jnp.bfloat16)
+            acc = combine_rows(acc, ret, idx, jnp.clip(filled - k * part, 0, part), k == CHUNKS - 1)
+        return acc
 
     row_spec = P(("dp", "ep"), None)
     weight_spec = P("ep", None, None)

time: 1020 us -> 1020 us (level)
  Pallas kernels: 111 us -> 126 us
    pallas_call x2, Pallas kernels: 69.1 us -> 83.4 us  [combine_rows(): pl.pallas_call(functools.partial(combine_kernel, last), grid_spec=pltpu.P...]
    unnamed x21 -> x20, local copies, waits for them, and re-layouts: 37.8 us -> 28.9 us
where the time goes in v5:
time: 1020 us; the launch traced here: 1010 us
  waiting for transfers between devices  551 us (54%)
  matrix products  255 us (25%)
  Pallas kernels  126 us (12%)
  local copies, waits for them, and re-layouts  29.6 us (3%)
  starting transfers between devices  27.9 us (3%)
  other arithmetic  19.9 us (2%)
    all_to_all x2, waiting for transfers between devices, local_layer(): lax.all_to_all(send.reshape((group_size, part) + tail), 'ep', 0, 0, tiled...  288 us
    all_to_all x2, waiting for transfers between devices, local_layer(): back.append((idx, lax.all_to_all(contrib, 'ep', 0, 0, tiled=True)))  263 us
    dot_general x2, matrix products, local_layer(): jnp.dot(got.reshape(rows, model_width), up_loc[0], preferred_element_type...  146 us
    dot_general x2, matrix products, local_layer(): out = jnp.dot(hidden, down_loc[0], preferred_element_type=jnp.float32)  110 us
    pallas_call x2, Pallas kernels, combine_rows(): pl.pallas_call(functools.partial(combine_kernel, last), grid_spec=pltpu.P...  83.4 us
    pallas_call x2, Pallas kernels, pack_rows(): pl.pallas_call(pack_kernel, grid_spec=pltpu.PrefetchScalarGridSpec(num_sc...  42.2 us
    unnamed x20, local copies, waits for them, and re-layouts  28.9 us
  transfers between devices with their start and end apart: 5, of which 4 were waited for; matrix products, arithmetic and copies ran while one was open for 29% of the time, Pallas kernels for 6%

profile of v5, /device:TPU:107, one launch (start us, length us, event | category | flops | bytes accessed | tf_op | source)
XLA Modules:
  0.0 1009.6 jit_solution(3099884260335454202)
XLA Ops:
  0.0 0.8 multiply_add_fusion.1
  1.1 0.2 convert_reduce_fusion
  1.4 0.8 concatenate.7
  2.2 6.4 sort.15
  8.6 0.7 broadcast_subtract_fusion
  9.3 7.7 all-to-all-start
  17.0 8.9 copy.9
  26.0 0.6 copy-done.3
  26.6 0.6 broadcast_minimum_fusion.1.idx_ref
  27.2 21.1 %shard_map.55 = bf16[8192,8,128]{2,1,0:T(8,128)(2,1)} custom-call(s32[8192]{0:T(1024)} %broadcast_minimum_fusion.1.idx_ref, bf16[4096,8,128]{2,1,0:T(8,128)(2,1)} %bitcast.75), custom_call_target="tpu_custom_call" | custom-call | flops 33554432 | bytes 33554432 | tf_op jit(solution)/shard_map/pallas_call | solution.py:34
  48.3 6.3 all-to-all-start.1
  54.7 0.6 copy.14
  55.4 0.6 copy-done.2
  56.0 0.6 broadcast_minimum_fusion.idx_ref
  56.6 21.1 %shard_map.57 = bf16[8192,8,128]{2,1,0:T(8,128)(2,1)} custom-call(s32[8192]{0:T(1024)} %broadcast_minimum_fusion.idx_ref, bf16[4096,8,128]{2,1,0:T(8,128)(2,1)} %bitcast.76), custom_call_target="tpu_custom_call" | custom-call | flops 33554432 | bytes 33554432 | tf_op jit(solution)/shard_map/pallas_call | solution.py:34
  77.7 200.2 %all-to-all-done.1 = bf16[32,256,8,128]{3,2,1,0:T(8,128)(2,1)} async-done(((bf16[32,256,8,128]{3,2,1,0:T(8,128)(2,1)}), bf16[32,256,8,128]{3,2,1,0:T(8,128)(2,1)}, u32[]{:S(2)}, u32[]{:S(2)}) %all-to-all-start.1) | async-done | bytes 16777248 | tf_op jit(solution)/shard_map/all_to_all | solution.py:137
  277.9 5.4 all-to-all-start.3
  283.3 72.8 %fusion.7.clone.6 = bf16[8192,2816]{1,0:T(8,128)(2,1)} fusion(bf16[1024,8,8,128]{3,2,1,0:T(8,128)(2,1)} %bitcast.15, bf16[1,1024,2816]{2,1,0:T(8,128)(2,1)} %param.8), kind=kOutput, calls=%fused_computation.9.clone.clone.clone.clone.clone.1 | convolution fusion | flops 47452258304 | bytes 68681728 | tf_op jit(solution)/shard_map/dot_general | solution.py:141
  356.1 55.0 %fusion.24 = bf16[1024,8,8,128]{3,1,2,0:T(8,128)(2,1)S(1)} fusion(f32[8192]{0:T(1024)S(1)} %bitcast.91, bf16[1,2816,1024]{2,1,0:T(8,128)(2,1)} %param.9, bf16[8192,2816]{1,0:T(8,128)(2,1)} %fusion.7.clone.6), kind=kOutput, calls=%fused_computation.24 | convolution fusion | flops 47261417472 | bytes 68714496 | tf_op jit(solution)/shard_map/dot_general | solution.py:142
  411.1 9.0 copy.12
  420.1 87.3 %all-to-all-done.3 = bf16[32,256,8,128]{3,2,1,0:T(8,128)(2,1)} async-done(((bf16[32,256,8,128]{3,2,1,0:T(8,128)(2,1)}), bf16[32,256,8,128]{3,2,1,0:T(8,128)(2,1)}, u32[]{:S(2)}, u32[]{:S(2)}) %all-to-all-start.3) | async-done | bytes 16777248 | tf_op jit(solution)/shard_map/all_to_all | solution.py:137
  507.4 4.5 all-to-all-start.2
  511.9 72.8 %fusion.15.clone.4 = bf16[8192,2816]{1,0:T(8,128)(2,1)} fusion(bf16[1024,8,8,128]{3,2,1,0:T(8,128)(2,1)} %bitcast.23, bf16[1,1024,2816]{2,1,0:T(8,128)(2,1)} %param.8), kind=kOutput, calls=%fused_computation.17.clone.clone.clone.clone.clone | convolution fusion | flops 47452258304 | bytes 68681728 | tf_op jit(solution)/shard_map/dot_general | solution.py:141
  584.7 54.9 %fusion.27 = bf16[1024,8,8,128]{3,1,2,0:T(8,128)(2,1)S(1)} fusion(f32[8192]{0:T(1024)S(1)} %bitcast.90, bf16[1,2816,1024]{2,1,0:T(8,128)(2,1)} %param.9, bf16[8192,2816]{1,0:T(8,128)(2,1)} %fusion.15.clone.4), kind=kOutput, calls=%fused_computation.25 | convolution fusion | flops 47261417472 | bytes 68714496 | tf_op jit(solution)/shard_map/dot_general | solution.py:142
  639.6 9.0 copy.15
  648.6 87.2 %all-to-all-done.2.ret_ref = bf16[32,256,8,128]{3,2,1,0:T(8,128)(2,1)} async-done(((bf16[32,256,8,128]{3,2,1,0:T(8,128)(2,1)}), bf16[32,256,8,128]{3,2,1,0:T(8,128)(2,1)}, u32[]{:S(2)}, u32[]{:S(2)}) %all-to-all-start.2) | async-done | bytes 16777248 | tf_op jit(solution)/shard_map/all_to_all | solution.py:145
  735.8 4.1 all-to-all-start.4
  739.9 9.5 bitcast_convert_fusion.base_ref
  749.5 0.5 broadcast_clamp_fusion
  750.0 36.5 %shard_map.56.base_ref = f32[4096,8,128]{2,1,0:T(8,128)} custom-call(s32[8192]{0:T(1024)} %bitcast.85, s32[32]{0:T(128)} %get-tuple-element.15.cnt_ref, f32[4096,8,128]{2,1,0:T(8,128)} %bitcast_convert_fusion.base_ref, bf16[32,256,8,128]{3,2,1,0:T(8,128)(2,1)} %all-to-all-done.2.ret_ref), custom_call_target="tpu_custom_call" | custom-call | flops 33554432 | bytes 50331648 | tf_op jit(solution)/shard_map/pallas_call | solution.py:88
  786.5 175.9 %all-to-all-done.4.ret_ref = bf16[32,256,8,128]{3,2,1,0:T(8,128)(2,1)} async-done(((bf16[32,256,8,128]{3,2,1,0:T(8,128)(2,1)}), bf16[32,256,8,128]{3,2,1,0:T(8,128)(2,1)}, u32[]{:S(2)}, u32[]{:S(2)}) %all-to-all-start.4) | async-done | bytes 16777248 | tf_op jit(solution)/shard_map/all_to_all | solution.py:145
  962.4 46.9 %shard_map.58 = bf16[4096,1024]{1,0:T(8,128)(2,1)} custom-call(s32[8192]{0:T(1024)} %bitcast.83, s32[32]{0:T(128)} %get-tuple-element.16.cnt_ref, f32[4096,8,128]{2,1,0:T(8,128)} %shard_map.56.base_ref, bf16[32,256,8,128]{3,2,1,0:T(8,128)(2,1)} %all-to-all-done.4.ret_ref), custom_call_target="tpu_custom_call" | custom-call | flops 33554432 | bytes 50331648 | tf_op jit(solution)/shard_map/pallas_call | solution.py:88
  (23 shorter events, 0.6 us)
Async XLA Ops:
  9.3 16.6 %all-to-all-start = ((s32[32,1,512]{2,1,0:T(1,128)}), s32[32,1,512]{2,1,0:T(1,128)S(1)}, u32[]{:S(2)}, u32[]{:S(2)}) async-start(s32[32,1,512]{2,1,0:T(1,128)} %broadcast_subtract_fusion), calls=%async_computation | async-start | bytes 131072 | tf_op jit(solution)/shard_map/all_to_all | solution.py:128
  26.0 51.7 %copy-start = (s32[32,1,512]{2,1,0:T(1,128)}, s32[32,1,512]{2,1,0:T(1,128)S(1)}, u32[]{:S(2)}) copy-start(s32[32,1,512]{2,1,0:T(1,128)S(1)} %all-to-all-done) | copy-start | bytes 196612
  26.0 0.6 copy-start.3
  48.3 229.6 %all-to-all-start.1 = ((bf16[32,256,8,128]{3,2,1,0:T(8,128)(2,1)}), bf16[32,256,8,128]{3,2,1,0:T(8,128)(2,1)}, u32[]{:S(2)}, u32[]{:S(2)}) async-start(bf16[32,256,8,128]{3,2,1,0:T(8,128)(2,1)} %bitcast.77), calls=%async_computation.1 | async-start | bytes 33554432 | tf_op jit(solution)/shard_map/all_to_all | solution.py:137
  55.4 0.6 copy-start.2
  277.9 229.5 %all-to-all-start.3 = ((bf16[32,256,8,128]{3,2,1,0:T(8,128)(2,1)}), bf16[32,256,8,128]{3,2,1,0:T(8,128)(2,1)}, u32[]{:S(2)}, u32[]{:S(2)}) async-start(bf16[32,256,8,128]{3,2,1,0:T(8,128)(2,1)} %bitcast.79), calls=%async_computation.3 | async-start | bytes 33554432 | tf_op jit(solution)/shard_map/all_to_all | solution.py:137
  507.4 228.4 %all-to-all-start.2 = ((bf16[32,256,8,128]{3,2,1,0:T(8,128)(2,1)}), bf16[32,256,8,128]{3,2,1,0:T(8,128)(2,1)}, u32[]{:S(2)}, u32[]{:S(2)}) async-start(bf16[32,256,8,128]{3,2,1,0:T(8,128)(2,1)} %bitcast.80), calls=%async_computation.2 | async-start | bytes 33554432 | tf_op jit(solution)/shard_map/all_to_all | solution.py:145
  511.9 72.8 %copy-start.4 = (f32[4,2,8,128]{3,1,2,0:T(2,128)S(1)}, f32[4,2,8,128]{3,1,2,0:T(2,128)}, u32[]{:S(2)}) copy-start(f32[4,2,8,128]{3,1,2,0:T(2,128)} %copy.14) | copy-start | bytes 98308
  648.6 100.8 %copy-start.1 = (s32[32,1,512]{2,1,0:T(1,128)S(1)}, s32[32,1,512]{2,1,0:T(1,128)}, u32[]{:S(2)}) copy-start(s32[32,1,512]{2,1,0:T(1,128)} %copy-done) | copy-start | bytes 196612
  735.8 226.6 %all-to-all-start.4 = ((bf16[32,256,8,128]{3,2,1,0:T(8,128)(2,1)}), bf16[32,256,8,128]{3,2,1,0:T(8,128)(2,1)}, u32[]{:S(2)}, u32[]{:S(2)}) async-start(bf16[32,256,8,128]{3,2,1,0:T(8,128)(2,1)} %bitcast.78), calls=%async_computation.4 | async-start | bytes 33554432 | tf_op jit(solution)/shard_map/all_to_all | solution.py:145
